TPU v7x, 32 devices: a whole 2x2x4 slice. The times are simulated.
32 devices in a mesh: gx: 4 (over z), gy: 2 (over y), gz: 4 (over x, core).
Axes of the slice: x: 2, y: 2, z: 4, core: 2. Of those that a mesh axis runs over, the one named last changes fastest.
Arguments:
- cell_volume: float32 [64, 32, 512], P('gx', 'gy', 'gz'), may hold values from 0.5 to 2
- exponent: int32 [64, 32, 512], P('gx', 'gy', 'gz'), may hold values from 0 to 7
- owner_row: int32 [8192], P(('gx', 'gy', 'gz')), may hold values from 0 to 8191, as said below
Outputs:
- stencil_out: float32 [27, 8192, 128], P(None, ('gx', 'gy', 'gz'))
- lumped_out: float32 [8192, 128], P(('gx', 'gy', 'gz'))
Inputs may be any that keep to these rules, and one draw needn't show every extreme that they name: owner_row is a permutation of the row blocks; the row blocks of each device's share of owner_row go to each owner (owner_row // 256) exactly 8 times.
All inputs are finite; a program needn't handle non-finite values.
Results may differ from a plain program's by a relative error of at most 0.00007.
Values sent between devices are 32-bit elements; how exact they have to be, the bound alone decides.
A program may use at most 64 MiB of HBM per device.

v0:
```python
import functools

import jax
import jax.numpy as jnp
from jax import lax
from jax.experimental import pallas as pl
from jax.experimental.pallas import tpu as pltpu
from jax.sharding import PartitionSpec as P

MESH = pl.DeviceIdType.MESH
AXES = ("gx", "gy", "gz")
F32, BF16, I32 = jnp.float32, jnp.bfloat16, jnp.int32
log_step = 0.3
NN = (((1,), (0,)), ((), ()))
NT = (((1,), (1,)), ((), ()))


def onehot(mask):
    return jnp.where(mask, 1.0, 0.0).astype(BF16)


def halves(x):
    hi = x.astype(BF16)
    return hi, (x - hi.astype(F32)).astype(BF16)


def pick(sel, x, dims=NN):
    total = None
    for part in halves(x):
        term = lax.dot_general(sel, part, dims, preferred_element_type=F32)
        total = term if total is None else total + term
    return total


def pick_r(x, sel, dims=NN):
    total = None
    for part in halves(x):
        term = lax.dot_general(part, sel, dims, preferred_element_type=F32)
        total = term if total is None else total + term
    return total


def iota(shape, dim):
    return lax.broadcasted_iota(I32, shape, dim)


def roll_lanes(x, shift):
    width = x.shape[1]
    cut = width - shift % width
    return jnp.concatenate([x[:, cut:], x[:, :cut]], axis=1)


def exchange(
    sizes, cv_hbm, ex_hbm, own_hbm, cur_ref, bef_ref,
    cv_ref, ex_ref, own_ref, in_sem,
    sb1, sb2, sb3, rb1, rb2, rb3, tx, ty, tc, tr, hx, hy, hc, hr,
    s_sem, r_sem, hs_sem, hr_sem,
):
    nx, ny, nz = sizes
    n = nx * ny * nz
    gx, gy, gz = (lax.axis_index(a) for a in AXES)
    me = (gx * ny + gy) * nz + gz
    sx, sy, width = cv_ref.shape
    lines = sx * sy
    s = lines // n

    def coords(d):
        return (d // (ny * nz), (d // nz) % ny, d % nz)

    arrive = []
    for i, (src, dst) in enumerate(((own_hbm, own_ref), (cv_hbm, cv_ref), (ex_hbm, ex_ref))):
        copy = pltpu.make_async_copy(src, dst, in_sem.at[i])
        copy.start()
        arrive.append(copy)
    barrier = pltpu.get_barrier_semaphore()

    def greet(k, carry):
        d = (me + k) % n
        pl.semaphore_signal(barrier, inc=1, device_id=coords(d), device_id_type=MESH)
        return carry

    lax.fori_loop(1, n, greet, 0)

    arrive[0].wait()
    owner_full = own_ref[...]
    owner = owner_full // lines
    slot = (owner_full % lines).astype(F32)
    mine = owner == iota((n, lines), 0)
    mine_b = onehot(mine)
    below = onehot(iota((lines, lines), 0) < iota((lines, lines), 1))
    counts = lax.dot_general(mine_b, below, NN, preferred_element_type=F32)
    rank = jnp.sum(jnp.where(mine, counts, 0.0), axis=0, keepdims=True).astype(I32)
    place = onehot(owner * s + rank == iota((lines, lines), 0))

    row_id = iota((width, lines), 0)
    at_rank = rank == row_id % s
    group = row_id // s

    arrive[1].wait()
    arrive[2].wait()
    w3 = cv_ref[...] * jnp.exp(-log_step * ex_ref[...].astype(F32))
    w = w3.reshape(lines, width)
    tx[...] = w[lines - sy :, :]
    ty[...] = w3[:, sy - 1 :, :]
    tc[...] = w[lines - 1 :, :]
    last = onehot(iota((8, width), 1) == width - 1)
    tr[...] = pick(last, w, NT)[0:1, :]

    packed0 = pick(place, w)
    sb1[:, 0:s, :] = packed0.reshape(n, s, width)
    slots = pick(mine_b, jnp.where(at_rank & (group == 0), slot, 0.0), NT)
    sb1[:, s : s + 1, :] = slots.reshape(n, 1, width)

    pl.semaphore_wait(barrier, n - 1)

    ux, uy, uz = (gx + 1) % nx, (gy + 1) % ny, (gz + 1) % nz
    halo = []
    routes = [
        (ty, hy, (gx, uy, gz)),
        (tx, hx, (ux, gy, gz)),
        (tc, hc, (ux, uy, gz)),
        (tr, hr.at[0], (gx, gy, uz)),
        (tr, hr.at[1], (ux, gy, uz)),
        (tr, hr.at[2], (gx, uy, uz)),
        (tr, hr.at[3], (ux, uy, uz)),
    ]
    for i, (src, dst, to) in enumerate(routes):
        copy = pltpu.make_async_remote_copy(
            src_ref=src, dst_ref=dst, send_sem=hs_sem.at[i], recv_sem=hr_sem.at[i],
            device_id=to, device_id_type=MESH,
        )
        copy.start()
        halo.append(copy)

    def send_all(stage, sb, rb):
        def send(k, carry):
            a, r = k // (ny * nz), k % (ny * nz)
            px, py, pz = (gx + a) % nx, (gy + r // nz) % ny, (gz + r % nz) % nz
            d = (px * ny + py) * nz + pz
            pltpu.make_async_remote_copy(
                src_ref=sb.at[d], dst_ref=rb.at[me], send_sem=s_sem.at[stage], recv_sem=r_sem.at[stage],
                device_id=coords(d), device_id_type=MESH,
            ).start()
            return carry

        lax.fori_loop(n // 2, n, send, 0)
        lax.fori_loop(ny * nz, n // 2, send, 0)
        lax.fori_loop(1, ny * nz, send, 0)
        pltpu.make_async_copy(sb.at[me], rb.at[me], r_sem.at[stage]).start()

    send_all(0, sb1, rb1)

    line_id = iota((lines, width), 0)
    first_j = line_id % sy == 0

    def back_j(x, edge):
        edge_full = jnp.broadcast_to(edge, (sx, sy, width)).reshape(lines, width)
        shifted = jnp.concatenate([x[lines - 1 :, :], x[: lines - 1, :]], axis=0)
        return jnp.where(first_j, edge_full, shifted)

    halo[0].wait()
    edge = hy[...]
    sb2[...] = pick(place, back_j(w, edge)).reshape(n, s, width)
    send_all(1, sb2, rb2)

    for copy in halo[1:]:
        copy.wait()
    x1 = jnp.concatenate([hx[...], w[: lines - sy, :]], axis=0)
    x3 = back_j(x1, jnp.concatenate([hc[...].reshape(1, 1, width), edge[: sx - 1]], axis=0))
    for c, x in enumerate((x1, x3)):
        sb3[:, c * s : (c + 1) * s, :] = pick(place, x).reshape(n, s, width)

    lane = iota((1, lines), 1)
    at_j0 = lane % sy == 0
    r0, rx, ry, rxy = hr[0], hr[1], hr[2], hr[3]
    rim1 = jnp.where(lane < sy, roll_lanes(rx, sy), roll_lanes(r0, sy))
    rim2 = jnp.where(at_j0, roll_lanes(ry, 1 - sy), roll_lanes(r0, 1))
    edge_rim = jnp.where(lane == 0, roll_lanes(rxy, 1), roll_lanes(ry, 1))
    rim3 = jnp.where(at_j0, edge_rim, roll_lanes(rim1, 1))
    rims = jnp.where(group == 0, r0, jnp.where(group == 1, rim1, jnp.where(group == 2, rim2, rim3)))
    rims = jnp.where(at_rank & (group < 4), rims, 0.0)
    sb3[:, 2 * s : 2 * s + 1, :] = pick(mine_b, rims, NT).reshape(n, 1, width)

    send_all(2, sb3, rb3)

    pltpu.make_async_copy(rb1, rb1, r_sem.at[0]).wait()
    col_id = iota((width, lines), 1)
    from_dev = iota((n, lines), 1) // s == iota((n, lines), 0)

    def spread(extra, q):
        sel = onehot(row_id == q * s + col_id % s)
        return jnp.sum(jnp.where(from_dev, pick_r(extra, sel), 0.0), axis=0, keepdims=True)

    slot_in = spread(rb1[:, s : s + 1, :].reshape(n, width), 0).astype(I32)
    to_slot = onehot(slot_in == iota((lines, lines), 0))
    cur_ref[0] = pick(to_slot, rb1[:, 0:s, :].reshape(lines, width))

    pltpu.make_async_copy(rb2, rb2, r_sem.at[1]).wait()
    cur_ref[2] = pick(to_slot, rb2[...].reshape(lines, width))

    pltpu.make_async_copy(rb3, rb3, r_sem.at[2]).wait()
    for c in range(2):
        cur_ref[2 * c + 1] = pick(to_slot, rb3[:, c * s : (c + 1) * s, :].reshape(lines, width))
    extra = rb3[:, 2 * s : 2 * s + 1, :].reshape(n, width)
    got = [spread(extra, q) for q in range(4)]
    rows = jnp.zeros((width, lines), F32)
    for q in range(4):
        rows = jnp.where(row_id == q, got[q], rows)
    bef_ref[...] = pick(to_slot, rows, NT)

    for stage, sb in enumerate((sb1, sb2, sb3)):
        sent = sb.at[pl.ds(0, n - 1)]
        pltpu.make_async_copy(sent, sent, s_sem.at[stage]).wait()


def finish(cur_ref, bef_ref, out_ref, lump_ref):
    shape = cur_ref.shape[1:]
    at_0 = iota(shape, 1) == 0
    near, far = [], []
    for c in range(4):
        x = cur_ref[c] * 0.015625
        shifted = pltpu.roll(x, 1, axis=1)
        near.append(x)
        far.append(jnp.where(at_0, bef_ref[:, c : c + 1] * 0.015625, shifted))

    def triple(c, b):
        return (b, 2.0 * (c + b), c)

    def nine(v):
        by_x0 = triple(v[0], v[1])
        by_x1 = triple(v[2], v[3])
        return [triple(by_x0[o1], by_x1[o1]) for o1 in range(3)]

    cur, back = nine(near), nine(far)
    for o1 in range(3):
        for o2 in range(3):
            for o3, value in enumerate(triple(cur[o1][o2], back[o1][o2])):
                out_ref[9 * o1 + 3 * o2 + o3] = value
    total = functools.reduce(lambda a, b: a + b, near + far)
    lump_ref[...] = 1.0 / (27.0 * total)


def shards(sizes, cell_volume, exponent, owner_row):
    sx, sy, width = cell_volume.shape
    lines = sx * sy
    n = sizes[0] * sizes[1] * sizes[2]
    s = lines // n
    vmem = pl.BlockSpec(memory_space=pltpu.VMEM)
    dma = pltpu.SemaphoreType.DMA
    cur, bef = pl.pallas_call(
        functools.partial(exchange, sizes),
        out_shape=(
            jax.ShapeDtypeStruct((4, lines, width), F32),
            jax.ShapeDtypeStruct((lines, width), F32),
        ),
        in_specs=[pl.BlockSpec(memory_space=pltpu.HBM)] * 3,
        out_specs=(vmem, vmem),
        scratch_shapes=[
            pltpu.VMEM((sx, sy, width), F32),
            pltpu.VMEM((sx, sy, width), I32),
            pltpu.VMEM((1, lines), I32),
            dma((3,)),
        ]
        + [pltpu.VMEM((n, rows, width), F32) for rows in (s + 1, s, 2 * s + 1)] * 2
        + [
            pltpu.VMEM((sy, width), F32),
            pltpu.VMEM((sx, 1, width), F32),
            pltpu.VMEM((1, width), F32),
            pltpu.VMEM((1, lines), F32),
            pltpu.VMEM((sy, width), F32),
            pltpu.VMEM((sx, 1, width), F32),
            pltpu.VMEM((1, width), F32),
            pltpu.VMEM((4, 1, lines), F32),
            dma((3,)),
            dma((3,)),
            dma((7,)),
            dma((7,)),
        ],
        compiler_params=pltpu.CompilerParams(
            collective_id=0, has_side_effects=True, vmem_limit_bytes=16 << 20
        ),
    )(*(pltpu.with_memory_space_constraint(a, pltpu.HBM) for a in (cell_volume, exponent, owner_row.reshape(1, lines))))
    rows = 128
    return pl.pallas_call(
        finish,
        grid=(lines // rows,),
        out_shape=(
            jax.ShapeDtypeStruct((27, lines, width), F32),
            jax.ShapeDtypeStruct((lines, width), F32),
        ),
        in_specs=[
            pl.BlockSpec((4, rows, width), lambda i: (0, i, 0)),
            pl.BlockSpec((rows, width), lambda i: (i, 0)),
        ],
        out_specs=(
            pl.BlockSpec((27, rows, width), lambda i: (0, i, 0)),
            pl.BlockSpec((rows, width), lambda i: (i, 0)),
        ),
        compiler_params=pltpu.CompilerParams(vmem_limit_bytes=16 << 20),
    )(cur, bef)


def solution(mesh):
    sizes = tuple(mesh.shape[a] for a in AXES)
    return jax.shard_map(
        functools.partial(shards, sizes),
        mesh=mesh,
        in_specs=(P(*AXES), P(*AXES), P(AXES)),
        out_specs=(P(None, AXES, None), P(AXES, None)),
        check_vma=False,
    )
```

profile of v0, /device:TPU:0, one launch (start us, length us, event | category | flops | bytes accessed | tf_op | source)
XLA Modules:
  0.0 23.4 jit_solution(7770030529289971404)
XLA Ops:
  0.6 20.6 %shard_map.50 = (f32[4,256,128]{2,1,0:T(8,128)S(1)}, f32[256,128]{1,0:T(8,128)S(1)}) custom-call(f32[16,16,128]{2,1,0:T(8,128)} %cv_hbm.1, s32[16,16,128]{2,1,0:T(8,128)} %ex_hbm.1, s32[1,256]{1,0:T(1,128)} %bitcast.1), custom_call_target="tpu_custom_call" | custom-call | tf_op jit(solution)/shard_map/pallas_call | solution.py:250
  21.2 2.1 %shard_map.51 = (f32[27,256,128]{2,1,0:T(8,128)}, f32[256,128]{1,0:T(8,128)}) custom-call(f32[4,256,128]{2,1,0:T(8,128)S(1)} %get-tuple-element.4.cur_ref, f32[256,128]{1,0:T(8,128)S(1)} %get-tuple-element.5.bef_ref), custom_call_target="tpu_custom_call" | custom-call | tf_op jit(solution)/shard_map/pallas_call | solution.py:284
where the time goes:
time: 23.5 us; the launch traced here: 23.4 us
  Pallas kernels  22.7 us (97%)
  between operations  0.64 us (3%)
    pallas_call x1, Pallas kernels, shards(): pl.pallas_call(functools.partial(exchange, sizes), out_shape=(jax.ShapeDt...  20.6 us
    pallas_call x1, Pallas kernels, shards(): pl.pallas_call(finish, grid=(lines // rows,), out_shape=(jax.ShapeDtypeSt...  2.14 us

commit v1 on v0

v1 whole, which is shorter than its diff:
```python
import functools

import jax
import jax.numpy as jnp
from jax import lax
from jax.experimental import pallas as pl
from jax.experimental.pallas import tpu as pltpu
from jax.sharding import PartitionSpec as P

MESH = pl.DeviceIdType.MESH
AXES = ("gx", "gy", "gz")
F32, BF16, I32 = jnp.float32, jnp.bfloat16, jnp.int32
log_step = 0.3
NN = (((1,), (0,)), ((), ()))
NT = (((1,), (1,)), ((), ()))


def onehot(mask):
    return jnp.where(mask, 1.0, 0.0).astype(BF16)


def halves(x):
    hi = x.astype(BF16)
    return hi, (x - hi.astype(F32)).astype(BF16)


def pick(sel, x, dims=NN):
    total = None
    for part in halves(x):
        term = lax.dot_general(sel, part, dims, preferred_element_type=F32)
        total = term if total is None else total + term
    return total


def pick_r(x, sel, dims=NN):
    total = None
    for part in halves(x):
        term = lax.dot_general(part, sel, dims, preferred_element_type=F32)
        total = term if total is None else total + term
    return total


def iota(shape, dim):
    return lax.broadcasted_iota(I32, shape, dim)


def roll_lanes(x, shift):
    width = x.shape[1]
    cut = width - shift % width
    return jnp.concatenate([x[:, cut:], x[:, :cut]], axis=1)


def exchange(
    sizes, cv_hbm, ex_hbm, own_hbm, cur_ref, bef_ref,
    cv_ref, ex_ref, own_ref, in_sem,
    sb1, sb2, rb1, rb2, tx, ty, tc, tr, hx, hy, hc, hr,
    s_sem, r_sem, hs_sem, hr_sem, ready,
):
    nx, ny, nz = sizes
    plane = ny * nz
    n = nx * plane
    gx, gy, gz = (lax.axis_index(a) for a in AXES)
    here = gy * nz + gz
    me = gx * plane + here
    sx, sy, width = cv_ref.shape
    lines = sx * sy
    s = lines // n
    spots = [(y, z) for y in range(ny) for z in range(nz)]
    ux, uy, uz = (gx + 1) % nx, (gy + 1) % ny, (gz + 1) % nz
    dx, dy, dz = (gx + nx - 1) % nx, (gy + ny - 1) % ny, (gz + nz - 1) % nz

    def signal(sem, to):
        pl.semaphore_signal(sem, inc=1, device_id=to, device_id_type=MESH)

    def others(visit):
        for y in range(ny):
            for z in range(nz):
                if y or z:
                    visit((gy + y) % ny, (gz + z) % nz)

    scope = jax.named_scope
    with scope("a_in"):
        arrive = []
        for i, (src, dst) in enumerate(((own_hbm, own_ref), (cv_hbm, cv_ref), (ex_hbm, ex_ref))):
            copy = pltpu.make_async_copy(src, dst, in_sem.at[i])
            copy.start()
            arrive.append(copy)
    with scope("b_bar"):
        barrier = pltpu.get_barrier_semaphore()
        others(lambda y, z: signal(barrier, (gx, y, z)))
        corners = [(dy, gz), (gy, dz), (dy, dz)]

        @pl.when(gx > 0)
        def _():
            for y, z in corners:
                signal(barrier, (dx, y, z))

        def greet_below(p, carry):
            signal(barrier, (p, gy, gz))
            return carry

        lax.fori_loop(0, gx, greet_below, 0)

        def greet_above(p, carry):
            for y, z in spots:
                signal(barrier, (p, y, z))
            return carry

        lax.fori_loop(gx + 1, nx, greet_above, 0)
        expect = plane - 1 + gx * plane + (nx - 1 - gx) + jnp.where(gx < nx - 1, len(corners), 0)

    with scope("c_own"):
        arrive[0].wait()
        owner_full = own_ref[...]
        owner = owner_full // lines
        slot = (owner_full % lines).astype(F32)
        mine = owner == iota((n, lines), 0)
        mine_b = onehot(mine)
        below = onehot(iota((lines, lines), 0) < iota((lines, lines), 1))
        counts = lax.dot_general(mine_b, below, NN, preferred_element_type=F32)
        rank = jnp.sum(jnp.where(mine, counts, 0.0), axis=0, keepdims=True).astype(I32)
        place = onehot(owner * s + rank == iota((lines, lines), 0))

        row_id = iota((width, lines), 0)
        at_rank = rank == row_id % s
        group = row_id // s

    with scope("d_inwait"):
        arrive[1].wait()
        arrive[2].wait()
    with scope("e_pack0"):
        w3 = cv_ref[...] * jnp.exp(-log_step * ex_ref[...].astype(F32))
        w = w3.reshape(lines, width)
        tx[...] = w[lines - sy :, :]
        ty[...] = w3[:, sy - 1 :, :]
        tc[...] = w[lines - 1 :, :]
        last = onehot(iota((8, width), 1) == width - 1)
        tr[...] = pick(last, w, NT)[0:1, :]
        sb1[...] = pick(place, w).reshape(n, s, width)

    with scope("g_barwait"):
        pl.semaphore_wait(barrier, expect)
        others(lambda y, z: signal(ready, (gx, y, z)))

    with scope("h_halosend"):
        halo = []
        routes = [
            (tx, hx, (ux, gy, gz)),
            (ty, hy, (gx, uy, gz)),
            (tc, hc, (ux, uy, gz)),
            (tr, hr.at[0], (gx, gy, uz)),
            (tr, hr.at[1], (ux, gy, uz)),
            (tr, hr.at[2], (gx, uy, uz)),
            (tr, hr.at[3], (ux, uy, uz)),
        ]
        for i, (src, dst, to) in enumerate(routes):
            copy = pltpu.make_async_remote_copy(
                src_ref=src, dst_ref=dst, send_sem=hs_sem.at[i], recv_sem=hr_sem.at[i],
                device_id=to, device_id_type=MESH,
            )
            copy.start()
            halo.append(copy)

    def send_one(stage, sb, rb, p, y, z):
        pltpu.make_async_remote_copy(
            src_ref=sb.at[p * plane + y * nz + z], dst_ref=rb.at[me], send_sem=s_sem.at[stage], recv_sem=r_sem.at[stage],
            device_id=(p, y, z), device_id_type=MESH,
        ).start()

    def send_below(stage, sb, rb):
        def send(p, carry):
            for y, z in spots:
                send_one(stage, sb, rb, p, y, z)
            return carry

        lax.fori_loop(0, gx, send, 0)

    def send_above(stage, sb, rb):
        def send(k, carry):
            for y, z in spots:
                send_one(stage, sb, rb, nx - 1 - k, y, z)
            return carry

        lax.fori_loop(0, nx - 1 - gx, send, 0)

    def send_plane(stage, sb, rb):
        others(lambda y, z: send_one(stage, sb, rb, gx, y, z))
        pltpu.make_async_copy(sb.at[me], rb.at[me], r_sem.at[stage]).start()

    with scope("i_send0"):
        send_below(0, sb1, rb1)
        send_plane(0, sb1, rb1)
    with scope("j_ready"):
        pl.semaphore_wait(ready, plane - 1)
    with scope("k_send0"):
        send_above(0, sb1, rb1)

    with scope("l_halo"):
        for copy in halo:
            copy.wait()

    with scope("m_pack1"):
        line_id = iota((lines, width), 0)
        first_j = line_id % sy == 0

        def back_j(x, edge):
            edge_full = jnp.broadcast_to(edge, (sx, sy, width)).reshape(lines, width)
            shifted = jnp.concatenate([x[lines - 1 :, :], x[: lines - 1, :]], axis=0)
            return jnp.where(first_j, edge_full, shifted)

        edge = hy[...]
        x1 = jnp.concatenate([hx[...], w[: lines - sy, :]], axis=0)
        x2 = back_j(w, edge)
        x3 = back_j(x1, jnp.concatenate([hc[...].reshape(1, 1, width), edge[: sx - 1]], axis=0))
        for c, x in enumerate((x1, x2, x3)):
            sb2[:, c * s : (c + 1) * s, :] = pick(place, x).reshape(n, s, width)

        lane = iota((1, lines), 1)
        at_j0 = lane % sy == 0
        r0, rx, ry, rxy = hr[0], hr[1], hr[2], hr[3]
        rim1 = jnp.where(lane < sy, roll_lanes(rx, sy), roll_lanes(r0, sy))
        rim2 = jnp.where(at_j0, roll_lanes(ry, 1 - sy), roll_lanes(r0, 1))
        edge_rim = jnp.where(lane == 0, roll_lanes(rxy, 1), roll_lanes(ry, 1))
        rim3 = jnp.where(at_j0, edge_rim, roll_lanes(rim1, 1))
        rims = slot
        for q, rim in enumerate((r0, rim1, rim2, rim3)):
            rims = jnp.where(group == q, rim, rims)
        rims = jnp.where(at_rank & (group < 5), rims, 0.0)
        sb2[:, 3 * s : 3 * s + 1, :] = pick(mine_b, rims, NT).reshape(n, 1, width)

    with scope("n_send1"):
        send_below(1, sb2, rb2)
        send_above(1, sb2, rb2)
        send_plane(1, sb2, rb2)

    with scope("q_wait"):
        pltpu.make_async_copy(rb1, rb1, r_sem.at[0]).wait()
        pltpu.make_async_copy(rb2, rb2, r_sem.at[1]).wait()
    with scope("r_unp"):
        extra = rb2[:, 3 * s : 3 * s + 1, :]
        spread = jnp.broadcast_to(extra, (n, s, width)).reshape(lines, width)
        spread = jnp.where(iota((lines, width), 1) % s == iota((lines, width), 0) % s, spread, 0.0)
        sums = onehot(iota((8, width), 1) // s == iota((8, width), 0))
        rows = pick(sums, spread, NT)
        to_slot = onehot(rows[4:5, :].astype(I32) == iota((lines, lines), 0))
        cur_ref[0] = pick(to_slot, rb1[...].reshape(lines, width))
        for c in range(3):
            cur_ref[c + 1] = pick(to_slot, rb2[:, c * s : (c + 1) * s, :].reshape(lines, width))
        bef_ref[...] = pick(to_slot, jnp.concatenate([rows, jnp.zeros((width - 8, lines), F32)], axis=0), NT)

    with scope("w_drain"):
        for stage, sb in enumerate((sb1, sb2)):
            sent = sb.at[pl.ds(0, n - 1)]
            pltpu.make_async_copy(sent, sent, s_sem.at[stage]).wait()


def finish(cur_ref, bef_ref, out_ref, lump_ref):
    shape = cur_ref.shape[1:]
    at_0 = iota(shape, 1) == 0
    near, far = [], []
    for c in range(4):
        x = cur_ref[c] * 0.015625
        shifted = pltpu.roll(x, 1, axis=1)
        near.append(x)
        far.append(jnp.where(at_0, bef_ref[:, c : c + 1] * 0.015625, shifted))

    def triple(c, b):
        return (b, 2.0 * (c + b), c)

    def nine(v):
        by_x0 = triple(v[0], v[1])
        by_x1 = triple(v[2], v[3])
        return [triple(by_x0[o1], by_x1[o1]) for o1 in range(3)]

    cur, back = nine(near), nine(far)
    for o1 in range(3):
        for o2 in range(3):
            for o3, value in enumerate(triple(cur[o1][o2], back[o1][o2])):
                out_ref[9 * o1 + 3 * o2 + o3] = value
    total = functools.reduce(lambda a, b: a + b, near + far)
    lump_ref[...] = 1.0 / (27.0 * total)


def shards(sizes, cell_volume, exponent, owner_row):
    sx, sy, width = cell_volume.shape
    lines = sx * sy
    n = sizes[0] * sizes[1] * sizes[2]
    s = lines // n
    vmem = pl.BlockSpec(memory_space=pltpu.VMEM)
    dma = pltpu.SemaphoreType.DMA
    cur, bef = pl.pallas_call(
        functools.partial(exchange, sizes),
        out_shape=(
            jax.ShapeDtypeStruct((4, lines, width), F32),
            jax.ShapeDtypeStruct((lines, width), F32),
        ),
        in_specs=[pl.BlockSpec(memory_space=pltpu.HBM)] * 3,
        out_specs=(vmem, vmem),
        scratch_shapes=[
            pltpu.VMEM((sx, sy, width), F32),
            pltpu.VMEM((sx, sy, width), I32),
            pltpu.VMEM((1, lines), I32),
            dma((3,)),
        ]
        + [pltpu.VMEM((n, rows, width), F32) for rows in (s, 3 * s + 1)] * 2
        + [
            pltpu.VMEM((sy, width), F32),
            pltpu.VMEM((sx, 1, width), F32),
            pltpu.VMEM((1, width), F32),
            pltpu.VMEM((1, lines), F32),
            pltpu.VMEM((sy, width), F32),
            pltpu.VMEM((sx, 1, width), F32),
            pltpu.VMEM((1, width), F32),
            pltpu.VMEM((4, 1, lines), F32),
            dma((2,)),
            dma((2,)),
            dma((7,)),
            dma((7,)),
            pltpu.SemaphoreType.REGULAR,
        ],
        compiler_params=pltpu.CompilerParams(
            collective_id=0, has_side_effects=True, vmem_limit_bytes=16 << 20
        ),
    )(*(pltpu.with_memory_space_constraint(a, pltpu.HBM) for a in (cell_volume, exponent, owner_row.reshape(1, lines))))
    rows = 128
    return pl.pallas_call(
        finish,
        grid=(lines // rows,),
        out_shape=(
            jax.ShapeDtypeStruct((27, lines, width), F32),
            jax.ShapeDtypeStruct((lines, width), F32),
        ),
        in_specs=[
            pl.BlockSpec((4, rows, width), lambda i: (0, i, 0)),
            pl.BlockSpec((rows, width), lambda i: (i, 0)),
        ],
        out_specs=(
            pl.BlockSpec((27, rows, width), lambda i: (0, i, 0)),
            pl.BlockSpec((rows, width), lambda i: (i, 0)),
        ),
        compiler_params=pltpu.CompilerParams(vmem_limit_bytes=16 << 20),
    )(cur, bef)


def solution(mesh):
    sizes = tuple(mesh.shape[a] for a in AXES)
    return jax.shard_map(
        functools.partial(shards, sizes),
        mesh=mesh,
        in_specs=(P(*AXES), P(*AXES), P(AXES)),
        out_specs=(P(None, AXES, None), P(AXES, None)),
        check_vma=False,
    )
```

time: 23.5 us -> 22.1 us (0.940)
  the two profiles are of different devices: /device:TPU:0 before, /device:TPU:21 now
where the time goes in v1:
time: 22.1 us; the launch traced here: 22 us
  Pallas kernels  21.3 us (96%)
  between operations  0.64 us (3%)
    pallas_call x1, Pallas kernels, shards(): pl.pallas_call(functools.partial(exchange, sizes), out_shape=(jax.ShapeDt...  19.2 us
    pallas_call x1, Pallas kernels, shards(): pl.pallas_call(finish, grid=(lines // rows,), out_shape=(jax.ShapeDtypeSt...  2.14 us

profile of v1, /device:TPU:21, one launch (start us, length us, event | category | flops | bytes accessed | tf_op | source)
XLA Modules:
  0.0 22.0 jit_solution(6201607018815261602)
XLA Ops:
  0.6 19.2 %shard_map.50 = (f32[4,256,128]{2,1,0:T(8,128)S(1)}, f32[256,128]{1,0:T(8,128)S(1)}) custom-call(f32[16,16,128]{2,1,0:T(8,128)} %cv_hbm.1, s32[16,16,128]{2,1,0:T(8,128)} %ex_hbm.1, s32[1,256]{1,0:T(1,128)} %bitcast.1), custom_call_target="tpu_custom_call" | custom-call | tf_op jit(solution)/shard_map/pallas_call | solution.py:291
  19.8 2.1 %shard_map.51 = (f32[27,256,128]{2,1,0:T(8,128)}, f32[256,128]{1,0:T(8,128)}) custom-call(f32[4,256,128]{2,1,0:T(8,128)S(1)} %get-tuple-element.4.cur_ref, f32[256,128]{1,0:T(8,128)S(1)} %get-tuple-element.5.bef_ref), custom_call_target="tpu_custom_call" | custom-call | tf_op jit(solution)/shard_map/pallas_call | solution.py:326

commit v2 on v1

v2 whole, which is shorter than its diff:
```python
import functools

import jax
import jax.numpy as jnp
from jax import lax
from jax.experimental import pallas as pl
from jax.experimental.pallas import tpu as pltpu
from jax.sharding import PartitionSpec as P

MESH = pl.DeviceIdType.MESH
AXES = ("gx", "gy", "gz")
F32, BF16, I32 = jnp.float32, jnp.bfloat16, jnp.int32
log_step = 0.3
NN = (((1,), (0,)), ((), ()))
NT = (((1,), (1,)), ((), ()))


def onehot(mask):
    return jnp.where(mask, 1.0, 0.0).astype(BF16)


def halves(x):
    hi = x.astype(BF16)
    return hi, (x - hi.astype(F32)).astype(BF16)


def pick(sel, x, dims=NN):
    total = None
    for part in halves(x):
        term = lax.dot_general(sel, part, dims, preferred_element_type=F32)
        total = term if total is None else total + term
    return total


def pick_r(x, sel, dims=NN):
    total = None
    for part in halves(x):
        term = lax.dot_general(part, sel, dims, preferred_element_type=F32)
        total = term if total is None else total + term
    return total


def iota(shape, dim):
    return lax.broadcasted_iota(I32, shape, dim)


def roll_lanes(x, shift):
    width = x.shape[1]
    cut = width - shift % width
    return jnp.concatenate([x[:, cut:], x[:, :cut]], axis=1)


def exchange(
    sizes, cv_hbm, ex_hbm, own_hbm, rb1, rb2,
    cv_ref, ex_ref, own_ref, in_sem,
    sb1, sb2, tx, ty, tc, tr, hx, hy, hc, hr,
    s_sem, r_sem, hs_sem, hr_sem, ready,
    vb1, vb2, wv, raw, raw_own, vx, vy, vc, vr, vs_sem, vr_sem,
):
    nx, ny, nz = sizes
    plane = ny * nz
    n = nx * plane
    gx, gy, gz = (lax.axis_index(a) for a in AXES)
    here = gy * nz + gz
    me = gx * plane + here
    sx, sy, width = cv_ref.shape
    lines = sx * sy
    s = lines // n
    relay = nx == 4
    half = n // 2
    base = (gx // 2) * 2
    middle = (gx == 1) | (gx == 2)
    across = (gx + 2) % nx
    theirs = across * plane + here
    spots = [(y, z) for y in range(ny) for z in range(nz)]
    ux, uy, uz = (gx + 1) % nx, (gy + 1) % ny, (gz + 1) % nz
    dx, dy, dz = (gx + nx - 1) % nx, (gy + ny - 1) % ny, (gz + nz - 1) % nz

    def signal(sem, to):
        pl.semaphore_signal(sem, inc=1, device_id=to, device_id_type=MESH)

    def others(visit):
        for y in range(ny):
            for z in range(nz):
                if y or z:
                    visit((gy + y) % ny, (gz + z) % nz)

    scope = jax.named_scope
    with scope("a_in"):
        arrive = []
        for i, (src, dst) in enumerate(((own_hbm, own_ref), (cv_hbm, cv_ref), (ex_hbm, ex_ref))):
            copy = pltpu.make_async_copy(src, dst, in_sem.at[i])
            copy.start()
            arrive.append(copy)
    with scope("b_bar"):
        barrier = pltpu.get_barrier_semaphore()
        others(lambda y, z: signal(barrier, (gx, y, z)))
        corners = [(dy, gz), (gy, dz), (dy, dz)]

        @pl.when(gx > 0)
        def _():
            for y, z in corners:
                signal(barrier, (dx, y, z))

        def greet_below(p, carry):
            signal(barrier, (p, gy, gz))
            return carry

        reach = 2 if relay else nx
        lax.fori_loop(jnp.maximum(gx - reach, 0), gx, greet_below, 0)

        def greet_above(p, carry):
            for y, z in spots:
                signal(barrier, (p, y, z))
            return carry

        lax.fori_loop(gx + 1, nx, greet_above, 0)
        expect = plane - 1 + gx * plane + jnp.minimum(nx - 1 - gx, reach) + jnp.where(gx < nx - 1, len(corners), 0)

    with scope("c_own"):
        arrive[0].wait()
        def ranks(own):
            owner = own // lines
            mine = owner == iota((n, lines), 0)
            counts = lax.dot_general(onehot(mine), below, NN, preferred_element_type=F32)
            rank = jnp.sum(jnp.where(mine, counts, 0.0), axis=0, keepdims=True).astype(I32)
            return onehot(mine), rank, owner * s + rank, (own % lines).astype(F32)

        below = onehot(iota((lines, lines), 0) < iota((lines, lines), 1))
        mine_b, rank, goes, slot = ranks(own_ref[...])
        place = onehot(goes == iota((lines, lines), 0))
        row_id = iota((width, lines), 0)
        group = row_id // s

    with scope("d_inwait"):
        arrive[1].wait()
        arrive[2].wait()
    with scope("e_pack0"):
        w3 = cv_ref[...] * jnp.exp(-log_step * ex_ref[...].astype(F32))
        w = w3.reshape(lines, width)
        wv[...] = w
        tx[...] = w[lines - sy :, :]
        ty[...] = w3[:, sy - 1 :, :]
        tc[...] = w[lines - 1 :, :]
        last = onehot(iota((8, width), 1) == width - 1)
        tr[...] = pick(last, w, NT)[0:1, :]
        sb1[...] = pick(place, w).reshape(n, s, width)

    with scope("g_barwait"):
        pl.semaphore_wait(barrier, expect)
        others(lambda y, z: signal(ready, (gx, y, z)))

    with scope("h_halosend"):
        halo = []
        routes = [
            (tx, hx, (ux, gy, gz)),
            (ty, hy, (gx, uy, gz)),
            (tc, hc, (ux, uy, gz)),
            (tr, hr.at[0], (gx, gy, uz)),
            (tr, hr.at[1], (ux, gy, uz)),
            (tr, hr.at[2], (gx, uy, uz)),
            (tr, hr.at[3], (ux, uy, uz)),
        ]
        for i, (src, dst, to) in enumerate(routes):
            copy = pltpu.make_async_remote_copy(
                src_ref=src, dst_ref=dst, send_sem=hs_sem.at[i], recv_sem=hr_sem.at[i],
                device_id=to, device_id_type=MESH,
            )
            copy.start()
            halo.append(copy)

    def hand(i, src, dst, to):
        return pltpu.make_async_remote_copy(
            src_ref=src, dst_ref=dst, send_sem=vs_sem.at[i], recv_sem=vr_sem.at[i], device_id=to, device_id_type=MESH
        )

    back = jnp.maximum(gx - 1, 0)
    raw_copies = [
        hand(1, own_ref, raw_own, (across, gy, gz)),
        hand(0, wv, raw, (across, gy, gz)),
    ]
    back_copies = [
        hand(2, tx, vx, (back, gy, gz)),
        hand(3, tc, vc, (back, uy, gz)),
        hand(4, tr, vr.at[1], (back, gy, uz)),
        hand(5, tr, vr.at[3], (back, uy, uz)),
    ]
    side_copies = [
        hand(6, ty, vy, (across, uy, gz)),
        hand(7, tr, vr.at[0], (across, gy, uz)),
        hand(8, tr, vr.at[2], (across, uy, uz)),
    ]

    def start_when(flag, copies):
        @pl.when(flag)
        def _():
            for copy in copies:
                copy.start()

    if relay:
        with scope("h_raw"):
            start_when(gx >= 2, back_copies)
            start_when(gx == nx - 1, side_copies + raw_copies)

    def send_one(stage, sb, rb, p, y, z):
        pltpu.make_async_remote_copy(
            src_ref=sb.at[p * plane + y * nz + z], dst_ref=rb.at[me], send_sem=s_sem.at[stage], recv_sem=r_sem.at[stage],
            device_id=(p, y, z), device_id_type=MESH,
        ).start()

    low, top = 0, nx - 1
    if relay:
        low, top = jnp.where(middle, 0, base), jnp.where(middle, nx - 1, base + 1)

    def send_below(stage, sb, rb):
        def send(p, carry):
            for y, z in spots:
                send_one(stage, sb, rb, p, y, z)
            return carry

        lax.fori_loop(low, gx, send, 0)

    def send_above(stage, sb, rb):
        def send(k, carry):
            for y, z in spots:
                send_one(stage, sb, rb, top - k, y, z)
            return carry

        lax.fori_loop(0, top - gx, send, 0)

    def send_plane(stage, sb, rb):
        others(lambda y, z: send_one(stage, sb, rb, gx, y, z))
        pltpu.make_async_copy(sb.at[me], rb.at[me], r_sem.at[stage]).start()

    with scope("i_send0"):
        send_below(0, sb1, rb1)
        send_plane(0, sb1, rb1)
    with scope("j_ready"):
        pl.semaphore_wait(ready, plane - 1)
    with scope("k_send0"):
        if relay:
            start_when(gx == 0, side_copies + raw_copies)
        send_above(0, sb1, rb1)

    with scope("l_halo"):
        for copy in halo:
            copy.wait()

    with scope("m_pack1"):
        line_id = iota((lines, width), 0)
        first_j = line_id % sy == 0
        lane = iota((1, lines), 1)
        at_j0 = lane % sy == 0

        def back_j(x, edge):
            edge_full = jnp.broadcast_to(edge, (sx, sy, width)).reshape(lines, width)
            shifted = jnp.concatenate([x[lines - 1 :, :], x[: lines - 1, :]], axis=0)
            return jnp.where(first_j, edge_full, shifted)

        def neighbours(w, hx, hy, hc):
            edge = hy[...]
            x1 = jnp.concatenate([hx[...], w[: lines - sy, :]], axis=0)
            x2 = back_j(w, edge)
            x3 = back_j(x1, jnp.concatenate([hc[...].reshape(1, 1, width), edge[: sx - 1]], axis=0))
            return x1, x2, x3

        def rim_rows(hr, mine_b, rank, slot):
            r0, rx, ry, rxy = hr[0], hr[1], hr[2], hr[3]
            rim1 = jnp.where(lane < sy, roll_lanes(rx, sy), roll_lanes(r0, sy))
            rim2 = jnp.where(at_j0, roll_lanes(ry, 1 - sy), roll_lanes(r0, 1))
            edge_rim = jnp.where(lane == 0, roll_lanes(rxy, 1), roll_lanes(ry, 1))
            rim3 = jnp.where(at_j0, edge_rim, roll_lanes(rim1, 1))
            rims = slot
            for q, rim in enumerate((r0, rim1, rim2, rim3)):
                rims = jnp.where(group == q, rim, rims)
            rims = jnp.where((rank == row_id % s) & (group < 5), rims, 0.0)
            return pick(mine_b, rims, NT)

        for c, x in enumerate(neighbours(w, hx, hy, hc)):
            sb2[:, c * s : (c + 1) * s, :] = pick(place, x).reshape(n, s, width)
        sb2[:, 3 * s : 3 * s + 1, :] = rim_rows(hr, mine_b, rank, slot).reshape(n, 1, width)

    with scope("n_send1"):
        send_below(1, sb2, rb2)
        send_above(1, sb2, rb2)
        send_plane(1, sb2, rb2)

    def send_theirs(stage, sb, rb):
        end = jnp.where(gx == 1, 0, nx - 1)

        def to(p, y, z):
            pltpu.make_async_remote_copy(
                src_ref=sb.at[(p - base) * plane + y * nz + z], dst_ref=rb.at[theirs],
                send_sem=vs_sem.at[9 + stage], recv_sem=r_sem.at[stage],
                device_id=(p, y, z), device_id_type=MESH,
            ).start()

        for y, z in spots:
            to(end, y, z)
        others(lambda y, z: to(gx, y, z))
        pltpu.make_async_copy(sb.at[(gx - base) * plane + here], rb.at[theirs], r_sem.at[stage]).start()

    if relay:

        @pl.when(middle)
        def _():
            with scope("o_wait0"):
                for copy in back_copies + side_copies:
                    copy.wait_recv()
                raw_copies[0].wait_recv()
            with scope("o_prep"):
                _, rank_v, goes_v, slot_v = ranks(raw_own[...])
                place_v = onehot(goes_v - base * plane * s == iota((lines // 2, lines), 0))
                mine_v = onehot(raw_own[...] // lines - base * plane == iota((half, lines), 0))
                vb2[:, 3 * s : 3 * s + 1, :] = rim_rows(vr, mine_v, rank_v, slot_v).reshape(half, 1, width)
            with scope("o_wait1"):
                raw_copies[1].wait_recv()
            with scope("o_pack"):
                x0 = raw[...]
                vb1[...] = pick(place_v, x0).reshape(half, s, width)
                for c, x in enumerate(neighbours(x0, vx, vy, vc)):
                    vb2[:, c * s : (c + 1) * s, :] = pick(place_v, x).reshape(half, s, width)
            with scope("o_send"):
                send_theirs(0, vb1, rb1)
                send_theirs(1, vb2, rb2)

    with scope("q_wait"):
        pltpu.make_async_copy(rb1, rb1, r_sem.at[0]).wait()
        pltpu.make_async_copy(rb2, rb2, r_sem.at[1]).wait()
    with scope("w_drain"):
        def sent(sb, count, sem):
            done = sb.at[pl.ds(0, count)]
            pltpu.make_async_copy(done, done, sem).wait()

        def drain(count):
            for stage, sb in enumerate((sb1, sb2)):
                sent(sb, count, s_sem.at[stage])

        if relay:

            @pl.when(middle)
            def _():
                drain(n - 1)
                for stage, sb in enumerate((vb1, vb2)):
                    sent(sb, half - 1, vs_sem.at[9 + stage])

            @pl.when(jnp.logical_not(middle))
            def _():
                drain(half - 1)
                for copy in raw_copies + side_copies:
                    copy.wait_send()

            @pl.when(gx >= 2)
            def _():
                for copy in back_copies:
                    copy.wait_send()

        else:
            drain(n - 1)


def finish(n, parts, rb1, rb2, out_hbm, lump_hbm, cur, bef, out_ref, lump_ref, sem):
    lines, width = lump_ref.shape
    s = lines // n
    extra = rb2[:, 3 * s : 3 * s + 1, :]
    spread = jnp.broadcast_to(extra, (n, s, width)).reshape(lines, width)
    spread = jnp.where(iota((lines, width), 1) % s == iota((lines, width), 0) % s, spread, 0.0)
    sums = onehot(iota((8, width), 1) // s == iota((8, width), 0))
    rows = pick(sums, spread, NT)
    slot = rows[4:5, :].astype(I32)
    rims = halves(jnp.concatenate([rows, jnp.zeros((width - 8, lines), F32)], axis=0))
    got = [halves(rb1[...].reshape(lines, width) * 0.015625)]
    got += [halves(rb2[:, c * s : (c + 1) * s, :].reshape(lines, width) * 0.015625) for c in range(3)]

    def triple(c, b):
        return (b, 2.0 * (c + b), c)

    def nine(v):
        by_x0 = triple(v[0], v[1])
        by_x1 = triple(v[2], v[3])
        return [triple(by_x0[o1], by_x1[o1]) for o1 in range(3)]

    def copies(first, count):
        part = pl.ds(first, count)
        return (
            pltpu.make_async_copy(out_ref.at[:, part, :], out_hbm.at[:, part, :], sem),
            pltpu.make_async_copy(lump_ref.at[part, :], lump_hbm.at[part, :], sem),
        )

    first = 0
    for count, piece in parts:
        to_slot = onehot(slot == iota((count, lines), 0) + first)
        for c in range(4):
            hi, lo = got[c]
            cur[c, first : first + count, :] = lax.dot_general(to_slot, hi, NN, preferred_element_type=F32) + lax.dot_general(
                to_slot, lo, NN, preferred_element_type=F32
            )
        hi, lo = rims
        bef[first : first + count, :] = lax.dot_general(to_slot, hi, NT, preferred_element_type=F32) + lax.dot_general(
            to_slot, lo, NT, preferred_element_type=F32
        )
        for start in range(first, first + count, piece):
            span = slice(start, start + piece)
            at_0 = iota((piece, width), 1) == 0
            near, far = [], []
            for c in range(4):
                x = cur[c, span, :]
                near.append(x)
                far.append(jnp.where(at_0, bef[span, c : c + 1] * 0.015625, pltpu.roll(x, 1, axis=1)))
            ahead, back = nine(near), nine(far)
            for o1 in range(3):
                for o2 in range(3):
                    for o3, value in enumerate(triple(ahead[o1][o2], back[o1][o2])):
                        out_ref[9 * o1 + 3 * o2 + o3, span, :] = value
            total = functools.reduce(lambda a, b: a + b, near + far)
            lump_ref[span, :] = 1.0 / (27.0 * total)
            for copy in copies(start, piece):
                copy.start()
        first += count
    for copy in copies(0, lines):
        copy.wait()


def shards(sizes, cell_volume, exponent, owner_row):
    sx, sy, width = cell_volume.shape
    lines = sx * sy
    n = sizes[0] * sizes[1] * sizes[2]
    s = lines // n
    vmem = pl.BlockSpec(memory_space=pltpu.VMEM)
    dma = pltpu.SemaphoreType.DMA
    rb1, rb2 = pl.pallas_call(
        functools.partial(exchange, sizes),
        out_shape=(
            jax.ShapeDtypeStruct((n, s, width), F32),
            jax.ShapeDtypeStruct((n, 3 * s + 1, width), F32),
        ),
        in_specs=[pl.BlockSpec(memory_space=pltpu.HBM)] * 3,
        out_specs=(vmem, vmem),
        scratch_shapes=[
            pltpu.VMEM((sx, sy, width), F32),
            pltpu.VMEM((sx, sy, width), I32),
            pltpu.VMEM((1, lines), I32),
            dma((3,)),
        ]
        + [pltpu.VMEM((n, rows, width), F32) for rows in (s, 3 * s + 1)]
        + [
            pltpu.VMEM((sy, width), F32),
            pltpu.VMEM((sx, 1, width), F32),
            pltpu.VMEM((1, width), F32),
            pltpu.VMEM((1, lines), F32),
            pltpu.VMEM((sy, width), F32),
            pltpu.VMEM((sx, 1, width), F32),
            pltpu.VMEM((1, width), F32),
            pltpu.VMEM((4, 1, lines), F32),
            dma((2,)),
            dma((2,)),
            dma((7,)),
            dma((7,)),
            pltpu.SemaphoreType.REGULAR,
        ]
        + [pltpu.VMEM((n // 2, rows, width), F32) for rows in (s, 3 * s + 1)]
        + [
            pltpu.VMEM((lines, width), F32),
            pltpu.VMEM((lines, width), F32),
            pltpu.VMEM((1, lines), I32),
            pltpu.VMEM((sy, width), F32),
            pltpu.VMEM((sx, 1, width), F32),
            pltpu.VMEM((1, width), F32),
            pltpu.VMEM((4, 1, lines), F32),
            dma((11,)),
            dma((9,)),
        ],
        compiler_params=pltpu.CompilerParams(
            collective_id=0, has_side_effects=True, vmem_limit_bytes=16 << 20
        ),
    )(*(pltpu.with_memory_space_constraint(a, pltpu.HBM) for a in (cell_volume, exponent, owner_row.reshape(1, lines))))
    parts = [(lines // 4, lines // 8)] * 4
    return pl.pallas_call(
        functools.partial(finish, n, parts),
        out_shape=(
            jax.ShapeDtypeStruct((27, lines, width), F32),
            jax.ShapeDtypeStruct((lines, width), F32),
        ),
        in_specs=[vmem, vmem],
        out_specs=(pl.BlockSpec(memory_space=pltpu.HBM), pl.BlockSpec(memory_space=pltpu.HBM)),
        scratch_shapes=[
            pltpu.VMEM((4, lines, width), F32),
            pltpu.VMEM((lines, width), F32),
            pltpu.VMEM((27, lines, width), F32),
            pltpu.VMEM((lines, width), F32),
            dma,
        ],
        compiler_params=pltpu.CompilerParams(vmem_limit_bytes=16 << 20),
    )(rb1, rb2)


def solution(mesh):
    sizes = tuple(mesh.shape[a] for a in AXES)
    return jax.shard_map(
        functools.partial(shards, sizes),
        mesh=mesh,
        in_specs=(P(*AXES), P(*AXES), P(AXES)),
        out_specs=(P(None, AXES, None), P(AXES, None)),
        check_vma=False,
    )
```

time: 22.1 us -> 21.2 us (0.959)
  the two profiles are of different devices: /device:TPU:21 before, /device:TPU:0 now
where the time goes in v2:
time: 21.2 us; the launch traced here: 21.1 us
  Pallas kernels  20.4 us (96%)
  between operations  0.64 us (3%)
    pallas_call x1, Pallas kernels, shards(): pl.pallas_call(functools.partial(exchange, sizes), out_shape=(jax.ShapeDt...  18.1 us
    pallas_call x1, Pallas kernels, shards(): pl.pallas_call(functools.partial(finish, n, parts), out_shape=(jax.ShapeD...  2.39 us

profile of v2, /device:TPU:0, one launch (start us, length us, event | category | flops | bytes accessed | tf_op | source)
XLA Modules:
  0.0 21.1 jit_solution(5684269143640465587)
XLA Ops:
  0.6 18.1 %shard_map.50 = (f32[32,8,128]{2,1,0:T(8,128)S(1)}, f32[32,25,128]{2,1,0:T(8,128)S(1)}) custom-call(f32[16,16,128]{2,1,0:T(8,128)} %cv_hbm.1, s32[16,16,128]{2,1,0:T(8,128)} %ex_hbm.1, s32[1,256]{1,0:T(1,128)} %bitcast.1), custom_call_target="tpu_custom_call" | custom-call | tf_op jit(solution)/shard_map/pallas_call | solution.py:431
  18.7 2.4 %shard_map.51 = (f32[27,256,128]{2,1,0:T(8,128)}, f32[256,128]{1,0:T(8,128)}) custom-call(f32[32,8,128]{2,1,0:T(8,128)S(1)} %get-tuple-element.4.rb1, f32[32,25,128]{2,1,0:T(8,128)S(1)} %get-tuple-element.5.rb2), custom_call_target="tpu_custom_call" | custom-call | tf_op jit(solution)/shard_map/pallas_call | solution.py:478

commit v3 on v2

--- a/solution.py
+++ b/solution.py
@@ -54,8 +54,8 @@
     sizes, cv_hbm, ex_hbm, own_hbm, rb1, rb2,
     cv_ref, ex_ref, own_ref, in_sem,
     sb1, sb2, tx, ty, tc, tr, hx, hy, hc, hr,
-    s_sem, r_sem, hs_sem, hr_sem, ready,
-    vb1, vb2, wv, raw, raw_own, vx, vy, vc, vr, vs_sem, vr_sem,
+    s_sem, r_sem, h_sem, v_sem, ready,
+    vb1, vb2, wv, raw, raw_own, vx, vy, vc, vr, tally,
 ):
     nx, ny, nz = sizes
     plane = ny * nz
@@ -70,8 +70,9 @@
     half = n // 2
     base = (gx // 2) * 2
     middle = (gx == 1) | (gx == 2)
-    across = (gx + 2) % nx
-    theirs = across * plane + here
+    across, beside = (gx + 2) % nx, jnp.where(gx < 2, 1 - gx, nx + 1 - gx)
+    give, take = jnp.where(middle, beside, across), jnp.where(middle, across, beside)
+    theirs = take * plane + here
     spots = [(y, z) for y in range(ny) for z in range(nz)]
     ux, uy, uz = (gx + 1) % nx, (gy + 1) % ny, (gz + 1) % nz
     dx, dy, dz = (gx + nx - 1) % nx, (gy + ny - 1) % ny, (gz + nz - 1) % nz
@@ -85,11 +86,18 @@
                 if y or z:
                     visit((gy + y) % ny, (gz + z) % nz)
 
+    def done(rows, sem):
+        part = tally.at[pl.ds(0, rows)]
+        pltpu.make_async_copy(part, part, sem).wait()
+
+    edge_rows = sx + sy + 1 + 4 * lines // width
+    pair_rows = 4 * s + 1
+
     scope = jax.named_scope
     with scope("a_in"):
         arrive = []
         for i, (src, dst) in enumerate(((own_hbm, own_ref), (cv_hbm, cv_ref), (ex_hbm, ex_ref))):
-            copy = pltpu.make_async_copy(src, dst, in_sem.at[i])
+            copy = pltpu.make_async_copy(src, dst, in_sem.at[min(i, 1)])
             copy.start()
             arrive.append(copy)
     with scope("b_bar"):
@@ -110,12 +118,25 @@
         lax.fori_loop(jnp.maximum(gx - reach, 0), gx, greet_below, 0)
 
         def greet_above(p, carry):
-            for y, z in spots:
-                signal(barrier, (p, y, z))
+            if relay:
+
+                @pl.when(p == 1)
+                def _():
+                    signal(barrier, (p, gy, gz))
+
+                @pl.when(p > 1)
+                def _():
+                    for y, z in spots:
+                        signal(barrier, (p, y, z))
+            else:
+                for y, z in spots:
+                    signal(barrier, (p, y, z))
             return carry
 
         lax.fori_loop(gx + 1, nx, greet_above, 0)
         expect = plane - 1 + gx * plane + jnp.minimum(nx - 1 - gx, reach) + jnp.where(gx < nx - 1, len(corners), 0)
+        if relay:
+            expect -= jnp.where(gx == 1, plane - 1, 0)
 
     with scope("c_own"):
         arrive[0].wait()
@@ -133,8 +154,7 @@
         group = row_id // s
 
     with scope("d_inwait"):
-        arrive[1].wait()
-        arrive[2].wait()
+        done(2 * lines, in_sem.at[1])
     with scope("e_pack0"):
         w3 = cv_ref[...] * jnp.exp(-log_step * ex_ref[...].astype(F32))
         w = w3.reshape(lines, width)
@@ -151,7 +171,6 @@
         others(lambda y, z: signal(ready, (gx, y, z)))
 
     with scope("h_halosend"):
-        halo = []
         routes = [
             (tx, hx, (ux, gy, gz)),
             (ty, hy, (gx, uy, gz)),
@@ -163,33 +182,18 @@
         ]
         for i, (src, dst, to) in enumerate(routes):
             copy = pltpu.make_async_remote_copy(
-                src_ref=src, dst_ref=dst, send_sem=hs_sem.at[i], recv_sem=hr_sem.at[i],
+                src_ref=src, dst_ref=dst, send_sem=s_sem, recv_sem=h_sem,
                 device_id=to, device_id_type=MESH,
             )
             copy.start()
-            halo.append(copy)
-
-    def hand(i, src, dst, to):
+
+    def hand(sem, src, dst):
         return pltpu.make_async_remote_copy(
-            src_ref=src, dst_ref=dst, send_sem=vs_sem.at[i], recv_sem=vr_sem.at[i], device_id=to, device_id_type=MESH
+            src_ref=src, dst_ref=dst, send_sem=s_sem, recv_sem=sem, device_id=(give, gy, gz), device_id_type=MESH
         )
 
-    back = jnp.maximum(gx - 1, 0)
-    raw_copies = [
-        hand(1, own_ref, raw_own, (across, gy, gz)),
-        hand(0, wv, raw, (across, gy, gz)),
-    ]
-    back_copies = [
-        hand(2, tx, vx, (back, gy, gz)),
-        hand(3, tc, vc, (back, uy, gz)),
-        hand(4, tr, vr.at[1], (back, gy, uz)),
-        hand(5, tr, vr.at[3], (back, uy, uz)),
-    ]
-    side_copies = [
-        hand(6, ty, vy, (across, uy, gz)),
-        hand(7, tr, vr.at[0], (across, gy, uz)),
-        hand(8, tr, vr.at[2], (across, uy, uz)),
-    ]
+    raw_copies = [hand(v_sem.at[0], own_ref, raw_own), hand(v_sem.at[1], wv, raw)]
+    edge_copies = [hand(v_sem.at[0], src, dst) for src, dst in ((hx, vx), (hy, vy), (hc, vc), (hr, vr))]
 
     def start_when(flag, copies):
         @pl.when(flag)
@@ -199,18 +203,18 @@
 
     if relay:
         with scope("h_raw"):
-            start_when(gx >= 2, back_copies)
-            start_when(gx == nx - 1, side_copies + raw_copies)
+            start_when(gx > 0, raw_copies)
 
     def send_one(stage, sb, rb, p, y, z):
         pltpu.make_async_remote_copy(
-            src_ref=sb.at[p * plane + y * nz + z], dst_ref=rb.at[me], send_sem=s_sem.at[stage], recv_sem=r_sem.at[stage],
+            src_ref=sb.at[p * plane + y * nz + z], dst_ref=rb.at[me], send_sem=s_sem, recv_sem=r_sem,
             device_id=(p, y, z), device_id_type=MESH,
         ).start()
 
     low, top = 0, nx - 1
     if relay:
-        low, top = jnp.where(middle, 0, base), jnp.where(middle, nx - 1, base + 1)
+        low = jnp.where(gx == 2, 0, jnp.where(gx == 1, 1, base))
+        top = jnp.where(gx == 1, nx - 1, jnp.where(gx == 2, 2, base + 1))
 
     def send_below(stage, sb, rb):
         def send(p, carry):
@@ -230,7 +234,7 @@
 
     def send_plane(stage, sb, rb):
         others(lambda y, z: send_one(stage, sb, rb, gx, y, z))
-        pltpu.make_async_copy(sb.at[me], rb.at[me], r_sem.at[stage]).start()
+        pltpu.make_async_copy(sb.at[me], rb.at[me], r_sem).start()
 
     with scope("i_send0"):
         send_below(0, sb1, rb1)
@@ -239,12 +243,14 @@
         pl.semaphore_wait(ready, plane - 1)
     with scope("k_send0"):
         if relay:
-            start_when(gx == 0, side_copies + raw_copies)
+            start_when(gx == 0, raw_copies)
         send_above(0, sb1, rb1)
 
     with scope("l_halo"):
-        for copy in halo:
-            copy.wait()
+        done(edge_rows, h_sem)
+        if relay:
+            for copy in edge_copies:
+                copy.start()
 
     with scope("m_pack1"):
         line_id = iota((lines, width), 0)
@@ -285,78 +291,61 @@
         send_above(1, sb2, rb2)
         send_plane(1, sb2, rb2)
 
-    def send_theirs(stage, sb, rb):
+    def send_theirs():
         end = jnp.where(gx == 1, 0, nx - 1)
+        pairs = ((vb1, rb1), (vb2, rb2))
 
         def to(p, y, z):
-            pltpu.make_async_remote_copy(
-                src_ref=sb.at[(p - base) * plane + y * nz + z], dst_ref=rb.at[theirs],
-                send_sem=vs_sem.at[9 + stage], recv_sem=r_sem.at[stage],
-                device_id=(p, y, z), device_id_type=MESH,
-            ).start()
-
-        for y, z in spots:
-            to(end, y, z)
-        others(lambda y, z: to(gx, y, z))
-        pltpu.make_async_copy(sb.at[(gx - base) * plane + here], rb.at[theirs], r_sem.at[stage]).start()
-
-    if relay:
+            for stage, (sb, rb) in enumerate(pairs):
+                pltpu.make_async_remote_copy(
+                    src_ref=sb.at[(p - base) * plane + y * nz + z], dst_ref=rb.at[theirs],
+                    send_sem=s_sem, recv_sem=r_sem,
+                    device_id=(p, y, z), device_id_type=MESH,
+                ).start()
 
         @pl.when(middle)
         def _():
-            with scope("o_wait0"):
-                for copy in back_copies + side_copies:
-                    copy.wait_recv()
-                raw_copies[0].wait_recv()
-            with scope("o_prep"):
-                _, rank_v, goes_v, slot_v = ranks(raw_own[...])
-                place_v = onehot(goes_v - base * plane * s == iota((lines // 2, lines), 0))
-                mine_v = onehot(raw_own[...] // lines - base * plane == iota((half, lines), 0))
-                vb2[:, 3 * s : 3 * s + 1, :] = rim_rows(vr, mine_v, rank_v, slot_v).reshape(half, 1, width)
-            with scope("o_wait1"):
-                raw_copies[1].wait_recv()
-            with scope("o_pack"):
-                x0 = raw[...]
-                vb1[...] = pick(place_v, x0).reshape(half, s, width)
-                for c, x in enumerate(neighbours(x0, vx, vy, vc)):
-                    vb2[:, c * s : (c + 1) * s, :] = pick(place_v, x).reshape(half, s, width)
-            with scope("o_send"):
-                send_theirs(0, vb1, rb1)
-                send_theirs(1, vb2, rb2)
+            for y, z in spots:
+                to(end, y, z)
+
+        others(lambda y, z: to(gx, y, z))
+        for stage, (sb, rb) in enumerate(pairs):
+            pltpu.make_async_copy(sb.at[(gx - base) * plane + here], rb.at[theirs], r_sem).start()
+
+    if relay:
+        with scope("o_wait0"):
+            done(edge_rows + lines // width, v_sem.at[0])
+        with scope("o_prep"):
+            _, rank_v, goes_v, slot_v = ranks(raw_own[...])
+            place_v = onehot(goes_v - base * plane * s == iota((lines // 2, lines), 0))
+            mine_v = onehot(raw_own[...] // lines - base * plane == iota((half, lines), 0))
+            vb2[:, 3 * s : 3 * s + 1, :] = rim_rows(vr, mine_v, rank_v, slot_v).reshape(half, 1, width)
+        with scope("o_wait1"):
+            done(lines, v_sem.at[1])
+        with scope("o_pack"):
+            x0 = raw[...]
+            vb1[...] = pick(place_v, x0).reshape(half, s, width)
+            for c, x in enumerate(neighbours(x0, vx, vy, vc)):
+                vb2[:, c * s : (c + 1) * s, :] = pick(place_v, x).reshape(half, s, width)
+        with scope("o_send"):
+            send_theirs()
 
     with scope("q_wait"):
-        pltpu.make_async_copy(rb1, rb1, r_sem.at[0]).wait()
-        pltpu.make_async_copy(rb2, rb2, r_sem.at[1]).wait()
+        done(n * pair_rows, r_sem)
     with scope("w_drain"):
-        def sent(sb, count, sem):
-            done = sb.at[pl.ds(0, count)]
-            pltpu.make_async_copy(done, done, sem).wait()
-
-        def drain(count):
-            for stage, sb in enumerate((sb1, sb2)):
-                sent(sb, count, s_sem.at[stage])
-
         if relay:
+            count = 2 * edge_rows + lines + lines // width
 
             @pl.when(middle)
             def _():
-                drain(n - 1)
-                for stage, sb in enumerate((vb1, vb2)):
-                    sent(sb, half - 1, vs_sem.at[9 + stage])
+                done(count + (n - plane - 1 + half - 1) * pair_rows, s_sem)
 
             @pl.when(jnp.logical_not(middle))
             def _():
-                drain(half - 1)
-                for copy in raw_copies + side_copies:
-                    copy.wait_send()
-
-            @pl.when(gx >= 2)
-            def _():
-                for copy in back_copies:
-                    copy.wait_send()
+                done(count + (half - 1 + plane - 1) * pair_rows, s_sem)
 
         else:
-            drain(n - 1)
+            done(edge_rows + (n - 1) * pair_rows, s_sem)
 
 
 def finish(n, parts, rb1, rb2, out_hbm, lump_hbm, cur, bef, out_ref, lump_ref, sem):
@@ -440,7 +429,7 @@
             pltpu.VMEM((sx, sy, width), F32),
             pltpu.VMEM((sx, sy, width), I32),
             pltpu.VMEM((1, lines), I32),
-            dma((3,)),
+            dma((2,)),
         ]
         + [pltpu.VMEM((n, rows, width), F32) for rows in (s, 3 * s + 1)]
         + [
@@ -452,10 +441,10 @@
             pltpu.VMEM((sx, 1, width), F32),
             pltpu.VMEM((1, width), F32),
             pltpu.VMEM((4, 1, lines), F32),
+            dma,
+            dma,
+            dma,
             dma((2,)),
-            dma((2,)),
-            dma((7,)),
-            dma((7,)),
             pltpu.SemaphoreType.REGULAR,
         ]
         + [pltpu.VMEM((n // 2, rows, width), F32) for rows in (s, 3 * s + 1)]
@@ -467,8 +456,7 @@
             pltpu.VMEM((sx, 1, width), F32),
             pltpu.VMEM((1, width), F32),
             pltpu.VMEM((4, 1, lines), F32),
-            dma((11,)),
-            dma((9,)),
+            pltpu.VMEM((2 * n * (4 * s + 1), width), F32),
         ],
         compiler_params=pltpu.CompilerParams(
             collective_id=0, has_side_effects=True, vmem_limit_bytes=16 << 20

time: 21.2 us -> 20.4 us (0.962)
  Pallas kernels: 20.4 us -> 19.6 us
    pallas_call x1, Pallas kernels: 18.1 us -> 17.2 us  [shards(): pl.pallas_call(functools.partial(exchange, sizes), out_shape=(jax.ShapeDt...]
where the time goes in v3:
time: 20.4 us; the launch traced here: 20.3 us
  Pallas kernels  19.6 us (96%)
  between operations  0.64 us (3%)
    pallas_call x1, Pallas kernels, shards(): pl.pallas_call(functools.partial(exchange, sizes), out_shape=(jax.ShapeDt...  17.2 us
    pallas_call x1, Pallas kernels, shards(): pl.pallas_call(functools.partial(finish, n, parts), out_shape=(jax.ShapeD...  2.39 us

profile of v3, /device:TPU:0, one launch (start us, length us, event | category | flops | bytes accessed | tf_op | source)
XLA Modules:
  0.0 20.3 jit_solution(16364820866237243314)
XLA Ops:
  0.6 17.2 %shard_map.50 = (f32[32,8,128]{2,1,0:T(8,128)S(1)}, f32[32,25,128]{2,1,0:T(8,128)S(1)}) custom-call(f32[16,16,128]{2,1,0:T(8,128)} %cv_hbm.1, s32[16,16,128]{2,1,0:T(8,128)} %ex_hbm.1, s32[1,256]{1,0:T(1,128)} %bitcast.1), custom_call_target="tpu_custom_call" | custom-call | tf_op jit(solution)/shard_map/pallas_call | solution.py:420
  17.9 2.4 %shard_map.51 = (f32[27,256,128]{2,1,0:T(8,128)}, f32[256,128]{1,0:T(8,128)}) custom-call(f32[32,8,128]{2,1,0:T(8,128)S(1)} %get-tuple-element.4.rb1, f32[32,25,128]{2,1,0:T(8,128)S(1)} %get-tuple-element.5.rb2), custom_call_target="tpu_custom_call" | custom-call | tf_op jit(solution)/shard_map/pallas_call | solution.py:466

commit v4 on v3

--- a/solution.py
+++ b/solution.py
@@ -51,11 +51,11 @@
 
 
 def exchange(
-    sizes, cv_hbm, ex_hbm, own_hbm, rb1, rb2,
+    sizes, cv_hbm, ex_hbm, own_hbm, rb,
     cv_ref, ex_ref, own_ref, in_sem,
-    sb1, sb2, tx, ty, tc, tr, hx, hy, hc, hr,
-    s_sem, r_sem, h_sem, v_sem, ready,
-    vb1, vb2, wv, raw, raw_own, vx, vy, vc, vr, tally,
+    sb, tx, ty, tc, tr, hx, hy, hc, hr,
+    s_sem, r_sem, h_sem, v_sem, ready, above,
+    vb, wv, raw, raw_own, vx, vy, vc, vr, tally,
 ):
     nx, ny, nz = sizes
     plane = ny * nz
@@ -114,7 +114,7 @@
             signal(barrier, (p, gy, gz))
             return carry
 
-        reach = 2 if relay else nx
+        reach = 1 if relay else nx
         lax.fori_loop(jnp.maximum(gx - reach, 0), gx, greet_below, 0)
 
         def greet_above(p, carry):
@@ -164,11 +164,17 @@
         tc[...] = w[lines - 1 :, :]
         last = onehot(iota((8, width), 1) == width - 1)
         tr[...] = pick(last, w, NT)[0:1, :]
-        sb1[...] = pick(place, w).reshape(n, s, width)
+        sb[:, 0:s, :] = pick(place, w).reshape(n, s, width)
 
     with scope("g_barwait"):
         pl.semaphore_wait(barrier, expect)
         others(lambda y, z: signal(ready, (gx, y, z)))
+        if relay:
+
+            @pl.when(gx == 1)
+            def _():
+                signal(above, (0, gy, gz))
+
 
     with scope("h_halosend"):
         routes = [
@@ -182,18 +188,32 @@
         ]
         for i, (src, dst, to) in enumerate(routes):
             copy = pltpu.make_async_remote_copy(
-                src_ref=src, dst_ref=dst, send_sem=s_sem, recv_sem=h_sem,
+                src_ref=src, dst_ref=dst, send_sem=s_sem, recv_sem=h_sem.at[0 if src is ty else 1],
                 device_id=to, device_id_type=MESH,
             )
             copy.start()
 
-    def hand(sem, src, dst):
+    def hand(sem, src, dst, to):
         return pltpu.make_async_remote_copy(
-            src_ref=src, dst_ref=dst, send_sem=s_sem, recv_sem=sem, device_id=(give, gy, gz), device_id_type=MESH
+            src_ref=src, dst_ref=dst, send_sem=s_sem, recv_sem=sem, device_id=to, device_id_type=MESH
         )
 
-    raw_copies = [hand(v_sem.at[0], own_ref, raw_own), hand(v_sem.at[1], wv, raw)]
-    edge_copies = [hand(v_sem.at[0], src, dst) for src, dst in ((hx, vx), (hy, vy), (hc, vc), (hr, vr))]
+    raw_copies = [hand(v_sem.at[2], own_ref, raw_own, (give, gy, gz)), hand(v_sem.at[1], wv, raw, (give, gy, gz))]
+    back = jnp.maximum(gx - 1, 0)
+    back_copies = [
+        hand(v_sem.at[0], tx, vx, (back, gy, gz)),
+        hand(v_sem.at[0], tc, vc, (back, uy, gz)),
+        hand(v_sem.at[0], tr, vr.at[1], (back, gy, uz)),
+        hand(v_sem.at[0], tr, vr.at[3], (back, uy, uz)),
+    ]
+    side_copies = [
+        hand(v_sem.at[0], ty, vy, (across, uy, gz)),
+        hand(v_sem.at[0], tr, vr.at[0], (across, gy, uz)),
+        hand(v_sem.at[0], tr, vr.at[2], (across, uy, uz)),
+    ]
+    edge_copies = [
+        hand(v_sem.at[0], src, dst, (give, gy, gz)) for src, dst in ((hx, vx), (hy, vy), (hc, vc), (hr, vr))
+    ]
 
     def start_when(flag, copies):
         @pl.when(flag)
@@ -203,9 +223,11 @@
 
     if relay:
         with scope("h_raw"):
+            start_when(gx >= 2, back_copies)
+            start_when(gx == nx - 1, side_copies)
             start_when(gx > 0, raw_copies)
 
-    def send_one(stage, sb, rb, p, y, z):
+    def send_one(p, y, z):
         pltpu.make_async_remote_copy(
             src_ref=sb.at[p * plane + y * nz + z], dst_ref=rb.at[me], send_sem=s_sem, recv_sem=r_sem,
             device_id=(p, y, z), device_id_type=MESH,
@@ -216,92 +238,111 @@
         low = jnp.where(gx == 2, 0, jnp.where(gx == 1, 1, base))
         top = jnp.where(gx == 1, nx - 1, jnp.where(gx == 2, 2, base + 1))
 
-    def send_below(stage, sb, rb):
+    def send_below():
         def send(p, carry):
             for y, z in spots:
-                send_one(stage, sb, rb, p, y, z)
+                send_one(p, y, z)
             return carry
 
         lax.fori_loop(low, gx, send, 0)
 
-    def send_above(stage, sb, rb):
+    def send_above():
         def send(k, carry):
             for y, z in spots:
-                send_one(stage, sb, rb, top - k, y, z)
+                send_one(top - k, y, z)
             return carry
 
         lax.fori_loop(0, top - gx, send, 0)
 
-    def send_plane(stage, sb, rb):
-        others(lambda y, z: send_one(stage, sb, rb, gx, y, z))
-        pltpu.make_async_copy(sb.at[me], rb.at[me], r_sem).start()
-
-    with scope("i_send0"):
-        send_below(0, sb1, rb1)
-        send_plane(0, sb1, rb1)
+    def send_plane(first, count):
+        def to(y, z):
+            d = gx * plane + y * nz + z
+            part = pl.ds(first, count)
+            pltpu.make_async_remote_copy(
+                src_ref=sb.at[d, part], dst_ref=rb.at[me, part], send_sem=s_sem, recv_sem=r_sem,
+                device_id=(gx, y, z), device_id_type=MESH,
+            ).start()
+
+        others(to)
+
+    split = 2 * s if (2 * s) % 8 == 0 else 0
+
     with scope("j_ready"):
         pl.semaphore_wait(ready, plane - 1)
     with scope("k_send0"):
         if relay:
-            start_when(gx == 0, raw_copies)
-        send_above(0, sb1, rb1)
-
-    with scope("l_halo"):
-        done(edge_rows, h_sem)
+
+            @pl.when(gx == 2)
+            def _():
+                signal(above, (1, gy, gz))
+
+            @pl.when(gx == 0)
+            def _():
+                pl.semaphore_wait(above, 1)
+
+            start_when(gx == 0, side_copies + raw_copies)
+
+    line_id = iota((lines, width), 0)
+    first_j = line_id % sy == 0
+    lane = iota((1, lines), 1)
+    at_j0 = lane % sy == 0
+
+    def back_j(x, edge):
+        edge_full = jnp.broadcast_to(edge, (sx, sy, width)).reshape(lines, width)
+        shifted = jnp.concatenate([x[lines - 1 :, :], x[: lines - 1, :]], axis=0)
+        return jnp.where(first_j, edge_full, shifted)
+
+    def behind_i(w, hx, hy, hc):
+        x1 = jnp.concatenate([hx[...], w[: lines - sy, :]], axis=0)
+        return x1, back_j(x1, jnp.concatenate([hc[...].reshape(1, 1, width), hy[...][: sx - 1]], axis=0))
+
+    def rim_rows(hr, mine_b, rank, slot):
+        r0, rx, ry, rxy = hr[0], hr[1], hr[2], hr[3]
+        rim1 = jnp.where(lane < sy, roll_lanes(rx, sy), roll_lanes(r0, sy))
+        rim2 = jnp.where(at_j0, roll_lanes(ry, 1 - sy), roll_lanes(r0, 1))
+        edge_rim = jnp.where(lane == 0, roll_lanes(rxy, 1), roll_lanes(ry, 1))
+        rim3 = jnp.where(at_j0, edge_rim, roll_lanes(rim1, 1))
+        rims = slot
+        for q, rim in enumerate((r0, rim1, rim2, rim3)):
+            rims = jnp.where(group == q, rim, rims)
+        rims = jnp.where((rank == row_id % s) & (group < 5), rims, 0.0)
+        return pick(mine_b, rims, NT)
+
+    with scope("l_halo0"):
+        done(sx, h_sem.at[0])
+    with scope("l_pack"):
+        sb[:, s : 2 * s, :] = pick(place, back_j(w, hy[...])).reshape(n, s, width)
+        if split:
+            send_plane(0, split)
+    with scope("l_halo1"):
+        done(edge_rows - sx, h_sem.at[1])
         if relay:
-            for copy in edge_copies:
-                copy.start()
-
+            start_when(middle, edge_copies)
     with scope("m_pack1"):
-        line_id = iota((lines, width), 0)
-        first_j = line_id % sy == 0
-        lane = iota((1, lines), 1)
-        at_j0 = lane % sy == 0
-
-        def back_j(x, edge):
-            edge_full = jnp.broadcast_to(edge, (sx, sy, width)).reshape(lines, width)
-            shifted = jnp.concatenate([x[lines - 1 :, :], x[: lines - 1, :]], axis=0)
-            return jnp.where(first_j, edge_full, shifted)
-
-        def neighbours(w, hx, hy, hc):
-            edge = hy[...]
-            x1 = jnp.concatenate([hx[...], w[: lines - sy, :]], axis=0)
-            x2 = back_j(w, edge)
-            x3 = back_j(x1, jnp.concatenate([hc[...].reshape(1, 1, width), edge[: sx - 1]], axis=0))
-            return x1, x2, x3
-
-        def rim_rows(hr, mine_b, rank, slot):
-            r0, rx, ry, rxy = hr[0], hr[1], hr[2], hr[3]
-            rim1 = jnp.where(lane < sy, roll_lanes(rx, sy), roll_lanes(r0, sy))
-            rim2 = jnp.where(at_j0, roll_lanes(ry, 1 - sy), roll_lanes(r0, 1))
-            edge_rim = jnp.where(lane == 0, roll_lanes(rxy, 1), roll_lanes(ry, 1))
-            rim3 = jnp.where(at_j0, edge_rim, roll_lanes(rim1, 1))
-            rims = slot
-            for q, rim in enumerate((r0, rim1, rim2, rim3)):
-                rims = jnp.where(group == q, rim, rims)
-            rims = jnp.where((rank == row_id % s) & (group < 5), rims, 0.0)
-            return pick(mine_b, rims, NT)
-
-        for c, x in enumerate(neighbours(w, hx, hy, hc)):
-            sb2[:, c * s : (c + 1) * s, :] = pick(place, x).reshape(n, s, width)
-        sb2[:, 3 * s : 3 * s + 1, :] = rim_rows(hr, mine_b, rank, slot).reshape(n, 1, width)
+        for c, x in enumerate(behind_i(w, hx, hy, hc)):
+            sb[:, (c + 2) * s : (c + 3) * s, :] = pick(place, x).reshape(n, s, width)
+        sb[:, 4 * s : 4 * s + 1, :] = rim_rows(hr, mine_b, rank, slot).reshape(n, 1, width)
 
     with scope("n_send1"):
-        send_below(1, sb2, rb2)
-        send_above(1, sb2, rb2)
-        send_plane(1, sb2, rb2)
+        send_below()
+        if relay:
+
+            @pl.when(gx == 1)
+            def _():
+                pl.semaphore_wait(above, 1)
+
+        send_above()
+        send_plane(split, pair_rows - split)
+        pltpu.make_async_copy(sb.at[me], rb.at[me], r_sem).start()
 
     def send_theirs():
         end = jnp.where(gx == 1, 0, nx - 1)
-        pairs = ((vb1, rb1), (vb2, rb2))
 
         def to(p, y, z):
-            for stage, (sb, rb) in enumerate(pairs):
-                pltpu.make_async_remote_copy(
-                    src_ref=sb.at[(p - base) * plane + y * nz + z], dst_ref=rb.at[theirs],
-                    send_sem=s_sem, recv_sem=r_sem,
-                    device_id=(p, y, z), device_id_type=MESH,
-                ).start()
+            pltpu.make_async_remote_copy(
+                src_ref=vb.at[(p - base) * plane + y * nz + z], dst_ref=rb.at[theirs], send_sem=s_sem, recv_sem=r_sem,
+                device_id=(p, y, z), device_id_type=MESH,
+            ).start()
 
         @pl.when(middle)
         def _():
@@ -309,24 +350,24 @@
                 to(end, y, z)
 
         others(lambda y, z: to(gx, y, z))
-        for stage, (sb, rb) in enumerate(pairs):
-            pltpu.make_async_copy(sb.at[(gx - base) * plane + here], rb.at[theirs], r_sem).start()
+        pltpu.make_async_copy(vb.at[(gx - base) * plane + here], rb.at[theirs], r_sem).start()
 
     if relay:
-        with scope("o_wait0"):
-            done(edge_rows + lines // width, v_sem.at[0])
         with scope("o_prep"):
+            done(lines // width, v_sem.at[2])
             _, rank_v, goes_v, slot_v = ranks(raw_own[...])
             place_v = onehot(goes_v - base * plane * s == iota((lines // 2, lines), 0))
             mine_v = onehot(raw_own[...] // lines - base * plane == iota((half, lines), 0))
-            vb2[:, 3 * s : 3 * s + 1, :] = rim_rows(vr, mine_v, rank_v, slot_v).reshape(half, 1, width)
+        with scope("o_wait0"):
+            done(edge_rows, v_sem.at[0])
+        with scope("o_rim"):
+            vb[:, 4 * s : 4 * s + 1, :] = rim_rows(vr, mine_v, rank_v, slot_v).reshape(half, 1, width)
         with scope("o_wait1"):
             done(lines, v_sem.at[1])
         with scope("o_pack"):
             x0 = raw[...]
-            vb1[...] = pick(place_v, x0).reshape(half, s, width)
-            for c, x in enumerate(neighbours(x0, vx, vy, vc)):
-                vb2[:, c * s : (c + 1) * s, :] = pick(place_v, x).reshape(half, s, width)
+            for c, x in enumerate((x0, back_j(x0, vy[...]), *behind_i(x0, vx, vy, vc))):
+                vb[:, c * s : (c + 1) * s, :] = pick(place_v, x).reshape(half, s, width)
         with scope("o_send"):
             send_theirs()
 
@@ -334,32 +375,37 @@
         done(n * pair_rows, r_sem)
     with scope("w_drain"):
         if relay:
-            count = 2 * edge_rows + lines + lines // width
+            count = edge_rows + lines + lines // width
+            back_rows = sy + 1 + 2 * lines // width
+
+            @pl.when(gx >= 2)
+            def _():
+                done(back_rows, s_sem)
+
 
             @pl.when(middle)
             def _():
-                done(count + (n - plane - 1 + half - 1) * pair_rows, s_sem)
+                done(count + edge_rows + (n - plane - 1 + half - 1) * pair_rows, s_sem)
 
             @pl.when(jnp.logical_not(middle))
             def _():
-                done(count + (half - 1 + plane - 1) * pair_rows, s_sem)
+                done(count + edge_rows - back_rows + (half - 1 + plane - 1) * pair_rows, s_sem)
 
         else:
             done(edge_rows + (n - 1) * pair_rows, s_sem)
 
 
-def finish(n, parts, rb1, rb2, out_hbm, lump_hbm, cur, bef, out_ref, lump_ref, sem):
+def finish(n, parts, rb, out_hbm, lump_hbm, cur, bef, out_ref, lump_ref, sem):
     lines, width = lump_ref.shape
     s = lines // n
-    extra = rb2[:, 3 * s : 3 * s + 1, :]
+    extra = rb[:, 4 * s : 4 * s + 1, :]
     spread = jnp.broadcast_to(extra, (n, s, width)).reshape(lines, width)
     spread = jnp.where(iota((lines, width), 1) % s == iota((lines, width), 0) % s, spread, 0.0)
     sums = onehot(iota((8, width), 1) // s == iota((8, width), 0))
     rows = pick(sums, spread, NT)
     slot = rows[4:5, :].astype(I32)
     rims = halves(jnp.concatenate([rows, jnp.zeros((width - 8, lines), F32)], axis=0))
-    got = [halves(rb1[...].reshape(lines, width) * 0.015625)]
-    got += [halves(rb2[:, c * s : (c + 1) * s, :].reshape(lines, width) * 0.015625) for c in range(3)]
+    got = [halves(rb[:, c * s : (c + 1) * s, :].reshape(lines, width) * 0.015625) for c in (0, 2, 1, 3)]
 
     def triple(c, b):
         return (b, 2.0 * (c + b), c)
@@ -417,22 +463,19 @@
     s = lines // n
     vmem = pl.BlockSpec(memory_space=pltpu.VMEM)
     dma = pltpu.SemaphoreType.DMA
-    rb1, rb2 = pl.pallas_call(
+    received = pl.pallas_call(
         functools.partial(exchange, sizes),
-        out_shape=(
-            jax.ShapeDtypeStruct((n, s, width), F32),
-            jax.ShapeDtypeStruct((n, 3 * s + 1, width), F32),
-        ),
+        out_shape=jax.ShapeDtypeStruct((n, 4 * s + 1, width), F32),
         in_specs=[pl.BlockSpec(memory_space=pltpu.HBM)] * 3,
-        out_specs=(vmem, vmem),
+        out_specs=vmem,
         scratch_shapes=[
             pltpu.VMEM((sx, sy, width), F32),
             pltpu.VMEM((sx, sy, width), I32),
             pltpu.VMEM((1, lines), I32),
             dma((2,)),
         ]
-        + [pltpu.VMEM((n, rows, width), F32) for rows in (s, 3 * s + 1)]
         + [
+            pltpu.VMEM((n, 4 * s + 1, width), F32),
             pltpu.VMEM((sy, width), F32),
             pltpu.VMEM((sx, 1, width), F32),
             pltpu.VMEM((1, width), F32),
@@ -443,12 +486,13 @@
             pltpu.VMEM((4, 1, lines), F32),
             dma,
             dma,
-            dma,
             dma((2,)),
+            dma((3,)),
+            pltpu.SemaphoreType.REGULAR,
             pltpu.SemaphoreType.REGULAR,
         ]
-        + [pltpu.VMEM((n // 2, rows, width), F32) for rows in (s, 3 * s + 1)]
         + [
+            pltpu.VMEM((n // 2, 4 * s + 1, width), F32),
             pltpu.VMEM((lines, width), F32),
             pltpu.VMEM((lines, width), F32),
             pltpu.VMEM((1, lines), I32),
@@ -469,7 +513,7 @@
             jax.ShapeDtypeStruct((27, lines, width), F32),
             jax.ShapeDtypeStruct((lines, width), F32),
         ),
-        in_specs=[vmem, vmem],
+        in_specs=[vmem],
         out_specs=(pl.BlockSpec(memory_space=pltpu.HBM), pl.BlockSpec(memory_space=pltpu.HBM)),
         scratch_shapes=[
             pltpu.VMEM((4, lines, width), F32),
@@ -479,7 +523,7 @@
             dma,
         ],
         compiler_params=pltpu.CompilerParams(vmem_limit_bytes=16 << 20),
-    )(rb1, rb2)
+    )(received)
 
 
 def solution(mesh):

time: 20.4 us -> 20 us (0.980)
  Pallas kernels: 19.6 us -> 19.2 us
    pallas_call x1, Pallas kernels: 17.2 us -> 16.8 us  [shards(): pl.pallas_call(functools.partial(exchange, sizes), out_shape=jax.ShapeDty...]
where the time goes in v4:
time: 20 us; the launch traced here: 19.8 us
  Pallas kernels  19.2 us (96%)
  between operations  0.64 us (3%)
    pallas_call x1, Pallas kernels, shards(): pl.pallas_call(functools.partial(exchange, sizes), out_shape=jax.ShapeDty...  16.8 us
    pallas_call x1, Pallas kernels, shards(): pl.pallas_call(functools.partial(finish, n, parts), out_shape=(jax.ShapeD...  2.39 us

profile of v4, /device:TPU:0, one launch (start us, length us, event | category | flops | bytes accessed | tf_op | source)
XLA Modules:
  0.0 19.8 jit_solution(17435449434707722162)
XLA Ops:
  0.6 16.8 %shard_map.50.rb = f32[32,33,128]{2,1,0:T(8,128)S(1)} custom-call(f32[16,16,128]{2,1,0:T(8,128)} %cv_hbm.1, s32[16,16,128]{2,1,0:T(8,128)} %ex_hbm.1, s32[1,256]{1,0:T(1,128)} %bitcast.1), custom_call_target="tpu_custom_call" | custom-call | tf_op jit(solution)/shard_map/pallas_call | solution.py:466
  17.4 2.4 %shard_map.51 = (f32[27,256,128]{2,1,0:T(8,128)}, f32[256,128]{1,0:T(8,128)}) custom-call(f32[32,33,128]{2,1,0:T(8,128)S(1)} %shard_map.50.rb), custom_call_target="tpu_custom_call" | custom-call | tf_op jit(solution)/shard_map/pallas_call | solution.py:510

commit v5 on v4

--- a/solution.py
+++ b/solution.py
@@ -215,6 +215,15 @@
         hand(v_sem.at[0], src, dst, (give, gy, gz)) for src, dst in ((hx, vx), (hy, vy), (hc, vc), (hr, vr))
     ]
 
+    def part_to(p, y, z, first, count):
+        d, part = p * plane + y * nz + z, pl.ds(first, count)
+        pltpu.make_async_remote_copy(
+            src_ref=sb.at[d, part], dst_ref=rb.at[me, part], send_sem=s_sem, recv_sem=r_sem,
+            device_id=(p, y, z), device_id_type=MESH,
+        ).start()
+
+    early = s if relay and s % 8 == 0 else 0
+
     def start_when(flag, copies):
         @pl.when(flag)
         def _():
@@ -226,6 +235,13 @@
             start_when(gx >= 2, back_copies)
             start_when(gx == nx - 1, side_copies)
             start_when(gx > 0, raw_copies)
+            if early:
+
+                @pl.when(gx == 2)
+                def _():
+                    for y, z in spots:
+                        part_to(0, y, z, 0, early)
+
 
     def send_one(p, y, z):
         pltpu.make_async_remote_copy(
@@ -244,7 +260,14 @@
                 send_one(p, y, z)
             return carry
 
-        lax.fori_loop(low, gx, send, 0)
+        if relay:
+
+            @pl.when(gx == 2)
+            def _():
+                for y, z in spots:
+                    part_to(0, y, z, early, pair_rows - early)
+
+        lax.fori_loop(jnp.maximum(low, 1) if relay else 0, gx, send, 0)
 
     def send_above():
         def send(k, carry):
@@ -255,15 +278,7 @@
         lax.fori_loop(0, top - gx, send, 0)
 
     def send_plane(first, count):
-        def to(y, z):
-            d = gx * plane + y * nz + z
-            part = pl.ds(first, count)
-            pltpu.make_async_remote_copy(
-                src_ref=sb.at[d, part], dst_ref=rb.at[me, part], send_sem=s_sem, recv_sem=r_sem,
-                device_id=(gx, y, z), device_id_type=MESH,
-            ).start()
-
-        others(to)
+        others(lambda y, z: part_to(gx, y, z, first, count))
 
     split = 2 * s if (2 * s) % 8 == 0 else 0
 
@@ -325,15 +340,15 @@
 
     with scope("n_send1"):
         send_below()
-        if relay:
-
-            @pl.when(gx == 1)
-            def _():
-                pl.semaphore_wait(above, 1)
-
-        send_above()
         send_plane(split, pair_rows - split)
         pltpu.make_async_copy(sb.at[me], rb.at[me], r_sem).start()
+        if relay:
+
+            @pl.when(gx == 1)
+            def _():
+                pl.semaphore_wait(above, 1)
+
+        send_above()
 
     def send_theirs():
         end = jnp.where(gx == 1, 0, nx - 1)

time: 20 us -> 19.9 us (level)
  no operation moved by 1% of the time
where the time goes in v5:
time: 19.9 us; the launch traced here: 19.8 us
  Pallas kernels  19.1 us (96%)
  between operations  0.64 us (3%)
    pallas_call x1, Pallas kernels, shards(): pl.pallas_call(functools.partial(exchange, sizes), out_shape=jax.ShapeDty...  16.8 us
    pallas_call x1, Pallas kernels, shards(): pl.pallas_call(functools.partial(finish, n, parts), out_shape=(jax.ShapeD...  2.39 us

profile of v5, /device:TPU:0, one launch (start us, length us, event | category | flops | bytes accessed | tf_op | source)
XLA Modules:
  0.0 19.8 jit_solution(17644871269566019173)
XLA Ops:
  0.6 16.8 %shard_map.50.rb = f32[32,33,128]{2,1,0:T(8,128)S(1)} custom-call(f32[16,16,128]{2,1,0:T(8,128)} %cv_hbm.1, s32[16,16,128]{2,1,0:T(8,128)} %ex_hbm.1, s32[1,256]{1,0:T(1,128)} %bitcast.1), custom_call_target="tpu_custom_call" | custom-call | tf_op jit(solution)/shard_map/pallas_call | solution.py:481
  17.4 2.4 %shard_map.51 = (f32[27,256,128]{2,1,0:T(8,128)}, f32[256,128]{1,0:T(8,128)}) custom-call(f32[32,33,128]{2,1,0:T(8,128)S(1)} %shard_map.50.rb), custom_call_target="tpu_custom_call" | custom-call | tf_op jit(solution)/shard_map/pallas_call | solution.py:525

commit v6 on v5

--- a/solution.py
+++ b/solution.py
@@ -92,6 +92,7 @@
 
     edge_rows = sx + sy + 1 + 4 * lines // width
     pair_rows = 4 * s + 1
+    down_rows = sx + 2 * lines // width
 
     scope = jax.named_scope
     with scope("a_in"):
@@ -122,7 +123,8 @@
 
                 @pl.when(p == 1)
                 def _():
-                    signal(barrier, (p, gy, gz))
+                    for y, z in [(gy, gz), *corners]:
+                        signal(barrier, (p, y, z))
 
                 @pl.when(p > 1)
                 def _():
@@ -136,7 +138,7 @@
         lax.fori_loop(gx + 1, nx, greet_above, 0)
         expect = plane - 1 + gx * plane + jnp.minimum(nx - 1 - gx, reach) + jnp.where(gx < nx - 1, len(corners), 0)
         if relay:
-            expect -= jnp.where(gx == 1, plane - 1, 0)
+            expect -= jnp.where(gx == 1, plane - 1 - len(corners), 0)
 
     with scope("c_own"):
         arrive[0].wait()
@@ -215,6 +217,13 @@
         hand(v_sem.at[0], src, dst, (give, gy, gz)) for src, dst in ((hx, vx), (hy, vy), (hc, vc), (hr, vr))
     ]
 
+    down_copies = [
+        hand(v_sem.at[0], ty, vy, (back, uy, gz)),
+        hand(v_sem.at[0], tr, vr.at[0], (back, gy, uz)),
+        hand(v_sem.at[0], tr, vr.at[2], (back, uy, uz)),
+    ]
+    flat_copies = [hand(v_sem.at[0], tc, vc, (gx, uy, gz))]
+
     def part_to(p, y, z, first, count):
         d, part = p * plane + y * nz + z, pl.ds(first, count)
         pltpu.make_async_remote_copy(
@@ -233,6 +242,8 @@
     if relay:
         with scope("h_raw"):
             start_when(gx >= 2, back_copies)
+            start_when(gx == 1, down_copies)
+            start_when(gx == 0, flat_copies)
             start_when(gx == nx - 1, side_copies)
             start_when(gx > 0, raw_copies)
             if early:
@@ -332,7 +343,7 @@
     with scope("l_halo1"):
         done(edge_rows - sx, h_sem.at[1])
         if relay:
-            start_when(middle, edge_copies)
+            start_when(gx == 2, edge_copies)
     with scope("m_pack1"):
         for c, x in enumerate(behind_i(w, hx, hy, hc)):
             sb[:, (c + 2) * s : (c + 3) * s, :] = pick(place, x).reshape(n, s, width)
@@ -374,7 +385,17 @@
             place_v = onehot(goes_v - base * plane * s == iota((lines // 2, lines), 0))
             mine_v = onehot(raw_own[...] // lines - base * plane == iota((half, lines), 0))
         with scope("o_wait0"):
-            done(edge_rows, v_sem.at[0])
+            @pl.when(gx == 0)
+            def _():
+                done(down_rows + 1, v_sem.at[0])
+                vx[...] = tx[...]
+                vr[1] = hr[0]
+                vr[3] = hr[2]
+
+            @pl.when(gx > 0)
+            def _():
+                done(edge_rows, v_sem.at[0])
+
         with scope("o_rim"):
             vb[:, 4 * s : 4 * s + 1, :] = rim_rows(vr, mine_v, rank_v, slot_v).reshape(half, 1, width)
         with scope("o_wait1"):
@@ -400,11 +421,19 @@
 
             @pl.when(middle)
             def _():
-                done(count + edge_rows + (n - plane - 1 + half - 1) * pair_rows, s_sem)
+                done(count + down_rows + (n - plane - 1 + half - 1) * pair_rows, s_sem)
+
+            @pl.when(gx == 2)
+            def _():
+                done(edge_rows - down_rows, s_sem)
+
+            @pl.when(gx == 0)
+            def _():
+                done(1, s_sem)
 
             @pl.when(jnp.logical_not(middle))
             def _():
-                done(count + edge_rows - back_rows + (half - 1 + plane - 1) * pair_rows, s_sem)
+                done(count + down_rows + (half - 1 + plane - 1) * pair_rows, s_sem)
 
         else:
             done(edge_rows + (n - 1) * pair_rows, s_sem)

time: 19.9 us -> 19.8 us (level)
  no operation moved by 1% of the time
where the time goes in v6:
time: 19.8 us; the launch traced here: 19.7 us
  Pallas kernels  19 us (96%)
  between operations  0.64 us (3%)
    pallas_call x1, Pallas kernels, shards(): pl.pallas_call(functools.partial(exchange, sizes), out_shape=jax.ShapeDty...  16.6 us
    pallas_call x1, Pallas kernels, shards(): pl.pallas_call(functools.partial(finish, n, parts), out_shape=(jax.ShapeD...  2.39 us

profile of v6, /device:TPU:0, one launch (start us, length us, event | category | flops | bytes accessed | tf_op | source)
XLA Modules:
  0.0 19.7 jit_solution(5570898772427098784)
XLA Ops:
  0.6 16.6 %shard_map.50.rb = f32[32,33,128]{2,1,0:T(8,128)S(1)} custom-call(f32[16,16,128]{2,1,0:T(8,128)} %cv_hbm.1, s32[16,16,128]{2,1,0:T(8,128)} %ex_hbm.1, s32[1,256]{1,0:T(1,128)} %bitcast.1), custom_call_target="tpu_custom_call" | custom-call | tf_op jit(solution)/shard_map/pallas_call | solution.py:510
  17.3 2.4 %shard_map.51 = (f32[27,256,128]{2,1,0:T(8,128)}, f32[256,128]{1,0:T(8,128)}) custom-call(f32[32,33,128]{2,1,0:T(8,128)S(1)} %shard_map.50.rb), custom_call_target="tpu_custom_call" | custom-call | tf_op jit(solution)/shard_map/pallas_call | solution.py:554
